TPU v7x, 32 devices: a 4x4x1 block of a 4x4x8 slice. The times are simulated.
32 devices in a mesh: dp: 1 (over z), sp: 4 (over y), tp: 8 (over x, core).
Axes of the slice: x: 4, y: 4, z: 1, core: 2. Of those that a mesh axis runs over, the one named last changes fastest.
The devices are a block of a 4x4x8 slice.
Arguments:
- hidden: bfloat16 [64, 5120], P('dp')
- new_pos: int32 [64], P('dp')
- k_self: bfloat16 [64, 256, 8, 128], P('dp', 'sp', 'tp')
- v_self: bfloat16 [64, 256, 8, 128], P('dp', 'sp', 'tp')
- k_cross: bfloat16 [64, 512, 8, 128], P('dp', None, 'tp')
- v_cross: bfloat16 [64, 512, 8, 128], P('dp', None, 'tp')
- xvalid: int32 [64, 512], P('dp')
- rowmask: int32 [64], P('dp')
- self_attn_norm: bfloat16 [5120], replicated
- self_wq: bfloat16 [5120, 4096], P(None, 'tp')
- self_wk: bfloat16 [5120, 1024], P(None, 'tp')
- self_wv: bfloat16 [5120, 1024], P(None, 'tp')
- self_wo: bfloat16 [4096, 5120], P('tp')
- self_mlp_norm: bfloat16 [5120], replicated
- self_wgate: bfloat16 [5120, 14336], P(None, 'tp')
- self_wup: bfloat16 [5120, 14336], P(None, 'tp')
- self_wdown: bfloat16 [14336, 5120], P('tp')
- cross_attn_norm: bfloat16 [5120], replicated
- cross_wq: bfloat16 [5120, 4096], P(None, 'tp')
- cross_qnorm: bfloat16 [128], replicated
- cross_wo: bfloat16 [4096, 5120], P('tp')
- cross_gates: float32 [2], replicated
- cross_mlp_norm: bfloat16 [5120], replicated
- cross_wgate: bfloat16 [5120, 14336], P(None, 'tp')
- cross_wup: bfloat16 [5120, 14336], P(None, 'tp')
- cross_wdown: bfloat16 [14336, 5120], P('tp')
Outputs:
- output 1: bfloat16 [64, 5120], P('dp')
- output 2: bfloat16 [64, 256, 8, 128], P('dp', 'sp', 'tp')
- output 3: bfloat16 [64, 256, 8, 128], P('dp', 'sp', 'tp')
All inputs are finite; a program needn't handle non-finite values.
Results may differ from a plain program's by a relative error of at most 0.0147858.
Values sent between devices are 32-bit elements.
A program may use at most 768 MiB of HBM per device.

v0:
```python
import math
import jax
import jax.numpy as jnp
from jax import lax
from jax.sharding import PartitionSpec as P

NORM_EPS = 1e-5
ROPE_THETA = 500000.0
ROPE_FACTOR = 8.0
LOW_FREQ = 1.0
HIGH_FREQ = 4.0
ORIG_CTX = 8192.0
NEG_BIG = -1e30


def rope_freqs(head_dim):
    inv_freq = 1.0 / (ROPE_THETA ** (jnp.arange(0, head_dim, 2).astype(jnp.float32) / head_dim))
    wavelen = 2.0 * math.pi / inv_freq
    smooth = (ORIG_CTX / wavelen - LOW_FREQ) / (HIGH_FREQ - LOW_FREQ)
    mid_freq = (1.0 - smooth) * inv_freq / ROPE_FACTOR + smooth * inv_freq
    scaled = jnp.where(wavelen > ORIG_CTX / LOW_FREQ, inv_freq / ROPE_FACTOR, mid_freq)
    return jnp.where(wavelen < ORIG_CTX / HIGH_FREQ, inv_freq, scaled)


def apply_rope(vectors, positions):
    head_dim = vectors.shape[-1]
    half_dim = head_dim // 2
    angles = positions.astype(jnp.float32)[:, None] * rope_freqs(head_dim)[None, :]
    cos_t = jnp.cos(angles)[:, None, :]
    sin_t = jnp.sin(angles)[:, None, :]
    first_half = vectors[..., :half_dim]
    second_half = vectors[..., half_dim:]
    return jnp.concatenate([first_half * cos_t - second_half * sin_t, second_half * cos_t + first_half * sin_t], axis=-1)


def rms_norm(values, gain_vec):
    vals32 = values.astype(jnp.float32)
    inv_rms = lax.rsqrt(jnp.mean(vals32 * vals32, axis=-1, keepdims=True) + NORM_EPS)
    return (vals32 * inv_rms * gain_vec.astype(jnp.float32)).astype(jnp.bfloat16)


def mlp_partial(normed, w_gate, w_up, w_down):
    gate_val = jnp.dot(normed, w_gate, preferred_element_type=jnp.float32).astype(jnp.bfloat16)
    up_val = jnp.dot(normed, w_up, preferred_element_type=jnp.float32).astype(jnp.bfloat16)
    hidden_act = (jax.nn.silu(gate_val.astype(jnp.float32)) * up_val.astype(jnp.float32)).astype(jnp.bfloat16)
    return jnp.dot(hidden_act, w_down, preferred_element_type=jnp.float32)


def local_softmax(queries, key_rows, val_rows, valid_mask, score_scale):
    scores = jnp.einsum('bkgd,btkd->bkgt', queries, key_rows, preferred_element_type=jnp.float32) * score_scale
    scores = jnp.where(valid_mask, scores, NEG_BIG)
    part_max = jnp.max(scores, axis=-1)
    probs_loc = jnp.where(valid_mask, jnp.exp(scores - part_max[..., None]), 0.0)
    part_sum = jnp.sum(probs_loc, axis=-1)
    part_out = jnp.einsum('bkgt,btkd->bkgd', probs_loc.astype(jnp.bfloat16), val_rows, preferred_element_type=jnp.float32)
    return part_max, part_sum, part_out


def combine_sp(part_max, part_sum, part_out):
    glob_max = lax.pmax(part_max, 'sp')
    factor = jnp.exp(part_max - glob_max)
    total_sum = lax.psum(part_sum * factor, 'sp')
    total_out = lax.psum(part_out * factor[..., None], 'sp')
    return total_out / total_sum[..., None]


def solution(mesh):
    cache_spec = P('dp', 'sp', 'tp', None)
    cross_spec = P('dp', None, 'tp', None)
    row_spec = P('dp', None)
    vec_spec = P('dp')
    full_spec = P(None)
    col_spec = P(None, 'tp')
    split_rows = P('tp', None)
    in_specs = (row_spec, vec_spec, cache_spec, cache_spec, cross_spec, cross_spec, row_spec, vec_spec,
                full_spec, col_spec, col_spec, col_spec, split_rows, full_spec, col_spec, col_spec, split_rows,
                full_spec, col_spec, full_spec, split_rows, full_spec, full_spec, col_spec, col_spec, split_rows)
    out_specs = (row_spec, cache_spec, cache_spec)

    def local_step(hidden, new_pos, k_self, v_self, k_cross, v_cross, xvalid, rowmask,
                   self_attn_norm, self_wq, self_wk, self_wv, self_wo, self_mlp_norm,
                   self_wgate, self_wup, self_wdown, cross_attn_norm, cross_wq, cross_qnorm,
                   cross_wo, cross_gates, cross_mlp_norm, cross_wgate, cross_wup, cross_wdown):
        batch_rows = hidden.shape[0]
        len_local = k_self.shape[1]
        kv_local = k_self.shape[2]
        head_dim = k_self.shape[3]
        heads_local = self_wq.shape[1] // head_dim
        group_size = heads_local // kv_local
        score_scale = head_dim ** -0.5
        normed = rms_norm(hidden, self_attn_norm)
        queries = jnp.dot(normed, self_wq, preferred_element_type=jnp.float32).astype(jnp.bfloat16)
        key_new = jnp.dot(normed, self_wk, preferred_element_type=jnp.float32).astype(jnp.bfloat16)
        val_new = jnp.dot(normed, self_wv, preferred_element_type=jnp.float32).astype(jnp.bfloat16)
        queries = apply_rope(queries.reshape(batch_rows, heads_local, head_dim).astype(jnp.float32), new_pos).astype(jnp.bfloat16)
        key_new = apply_rope(key_new.reshape(batch_rows, kv_local, head_dim).astype(jnp.float32), new_pos).astype(jnp.bfloat16)
        val_new = val_new.reshape(batch_rows, kv_local, head_dim)
        local_pos = new_pos - lax.axis_index('sp') * len_local
        slot_ids = jnp.arange(len_local)
        hit_mask = (slot_ids[None, :] == local_pos[:, None])[:, :, None, None]
        k_new_cache = jnp.where(hit_mask, key_new[:, None], k_self)
        v_new_cache = jnp.where(hit_mask, val_new[:, None], v_self)
        seen_mask = (slot_ids[None, :] <= local_pos[:, None])[:, None, None, :]
        self_stats = local_softmax(queries.reshape(batch_rows, kv_local, group_size, head_dim), k_new_cache, v_new_cache, seen_mask, score_scale)
        self_attn = combine_sp(self_stats[0], self_stats[1], self_stats[2])
        self_flat = self_attn.astype(jnp.bfloat16).reshape(batch_rows, heads_local * head_dim)
        attn_sum = lax.psum(jnp.dot(self_flat, self_wo, preferred_element_type=jnp.float32), 'tp')
        after_attn = (hidden.astype(jnp.float32) + attn_sum).astype(jnp.bfloat16)
        mlp_sum = lax.psum(mlp_partial(rms_norm(after_attn, self_mlp_norm), self_wgate, self_wup, self_wdown), 'tp')
        after_mlp = (after_attn.astype(jnp.float32) + mlp_sum).astype(jnp.bfloat16)
        normed = rms_norm(after_mlp, cross_attn_norm)
        cross_q = jnp.dot(normed, cross_wq, preferred_element_type=jnp.float32).astype(jnp.bfloat16)
        cross_q = rms_norm(cross_q.reshape(batch_rows, heads_local, head_dim), cross_qnorm)
        cross_mask = (xvalid > 0)[:, None, None, :]
        cross_stats = local_softmax(cross_q.reshape(batch_rows, kv_local, group_size, head_dim), k_cross, v_cross, cross_mask, score_scale)
        cross_attn = cross_stats[2] / cross_stats[1][..., None]
        cross_flat = cross_attn.astype(jnp.bfloat16).reshape(batch_rows, heads_local * head_dim)
        gate_vals = jnp.tanh(cross_gates.astype(jnp.float32))
        row_scale = rowmask.astype(jnp.float32)[:, None]
        xattn_sum = lax.psum(jnp.dot(cross_flat, cross_wo, preferred_element_type=jnp.float32), 'tp')
        after_cross = (after_mlp.astype(jnp.float32) + gate_vals[0] * row_scale * xattn_sum).astype(jnp.bfloat16)
        xmlp_sum = lax.psum(mlp_partial(rms_norm(after_cross, cross_mlp_norm), cross_wgate, cross_wup, cross_wdown), 'tp')
        after_xmlp = (after_cross.astype(jnp.float32) + gate_vals[1] * row_scale * xmlp_sum).astype(jnp.bfloat16)
        return after_xmlp, k_new_cache, v_new_cache

    return jax.shard_map(local_step, mesh=mesh, in_specs=in_specs, out_specs=out_specs, check_vma=False)
```

profile of v0, /device:TPU:97, one launch (start us, length us, event | category | flops | bytes accessed | tf_op | source)
XLA Modules:
  0.0 401.1 jit_solution(11678093263067751570)
XLA Ops:
  8.1 1.5 fusion.13
  10.5 1.5 fusion.49
  12.7 3.6 fusion.38
  16.7 3.4 broadcast_select_fusion.1
  21.1 16.1 %pmax.7 = f32[64,1,4]{2,0,1:T(8,128)S(1)} all-reduce(f32[64,1,4]{2,0,1:T(8,128)S(1)} %bitcast.74), channel_id=1, replica_groups=mesh['dp'=1,'sp'=4,'tp'=8] {'sp'}, use_global_device_ids=true, to_apply=%region_2.3 | all-reduce | flops 256 | bytes 2048 | tf_op jit(solution)/shard_map/pmax | solution.py:60
  38.4 11.1 %psum.43 = f32[64,4]{1,0:T(8,128)S(1)} all-reduce(f32[64,4]{1,0:T(8,128)S(1)} %get-tuple-element.11), channel_id=1, replica_groups=mesh['dp'=1,'sp'=4,'tp'=8] {'sp'}, use_global_device_ids=true, to_apply=%region_5.6 | all-reduce | flops 256 | bytes 2048 | tf_op jit(solution)/shard_map/psum | solution.py:62
  49.5 26.9 %all-reduce.6.cloned.1.call-done = f32[64,1,4,128]{3,2,0,1:T(4,128)} async-done(((f32[64,1,4,128]{3,2,0,1:T(4,128)}), f32[64,1,4,128]{3,2,0,1:T(4,128)}) %all-reduce.6.cloned.1.call-update) | async-done | bytes 131088 | tf_op jit(solution)/shard_map/psum | solution.py:63
  77.5 4.6 %fusion.82 = f32[64,5120]{1,0:T(8,128)} fusion(bf16[512,5120]{1,0:T(8,128)(2,1)} %param.38, bf16[8,8,4,128]{3,2,1,0:T(4,128)(2,1)S(1)} %bitcast.75), kind=kOutput, calls=%fused_computation.96 | convolution fusion | flops 335544320 | bytes 6619136 | tf_op jit(solution)/shard_map/dot_general | solution.py:107
  82.8 58.0 %all-reduce.8.cloned.1.call-done = f32[64,5120]{1,0:T(8,128)} async-done(((f32[64,5120]{1,0:T(8,128)}), f32[64,5120]{1,0:T(8,128)}) %all-reduce.8.cloned.1.call-update) | async-done | bytes 1310736 | tf_op jit(solution)/shard_map/psum | solution.py:107
  140.8 1.6 fusion.17
  142.5 9.6 %fusion.12 = f32[64,1792]{1,0:T(8,128)S(1)} fusion(bf16[5120,1792]{1,0:T(8,128)(2,1)} %param.40, bf16[64,5120]{1,0:T(8,128)(2,1)S(1)} %get-tuple-element.8, f32[5120]{0:T(1024)S(1)} %convert_element_type.180, f32[64]{0:T(128)S(1)} %add_rsqrt_fusion.3), kind=kOutput, calls=%fused_computation.16 | convolution fusion | flops 1175945216 | bytes 19484928 | tf_op jit(solution)/shard_map/dot_general | solution.py:43
  152.0 18.7 %fusion.55 = f32[64,5120]{1,0:T(8,128)} fusion(bf16[1792,5120]{1,0:T(8,128)(2,1)} %param.42, bf16[5120,1792]{1,0:T(8,128)(2,1)} %param.41, f32[64,1792]{1,0:T(8,128)S(1)} %fusion.12, bf16[64,5120]{1,0:T(8,128)(2,1)S(1)} %get-tuple-element.8, f32[5120]{0:T(1024)S(1)} %convert_element_type.180, f32[64]{0:T(128)S(1)} %add_rsqrt_fusion.3), kind=kOutput, calls=%fused_computation.70 | convolution fusion | flops 2351038464 | bytes 39145728 | tf_op jit(solution)/shard_map/dot_general | solution.py:46
  171.7 56.7 %all-reduce.10.cloned.1.call-done = f32[64,5120]{1,0:T(8,128)} async-done(((f32[64,5120]{1,0:T(8,128)}), f32[64,5120]{1,0:T(8,128)}) %all-reduce.10.cloned.1.call-update) | async-done | bytes 1310736 | tf_op jit(solution)/shard_map/psum | solution.py:109
  228.5 1.6 fusion.21
  230.1 3.6 fusion.37
  233.9 6.0 %fusion.118 = (f32[64,4]{1,0:T(8,128)S(1)}, bf16[64,4,512]{2,1,0:T(4,128)(2,1)S(1)}) fusion(pred[64,512]{1,0:T(8,128)(4,1)S(1)} %broadcast_compare_fusion, bf16[64,512,1,128]{3,1,2,0:T(8,128)(2,1)} %param.30, f32[64,4,128]{2,1,0:T(4,128)S(1)} %reshape.337, f32[128]{0:T(128)S(1)} %convert_element_type.195, f32[64,4]{1,0:T(8,128)S(1)} %add_rsqrt_fusion), kind=kOutput, calls=%fused_computation.146 | convolution fusion | flops 34439680 | bytes 8817152 | tf_op jit(solution)/shard_map/sub | solution.py:53
  239.8 4.7 %fusion.42 = bf16[64,4,128]{2,1,0:T(4,128)(2,1)S(1)} fusion(bf16[64,512,1,128]{3,1,2,0:T(8,128)(2,1)} %param.31, bf16[64,4,512]{2,1,0:T(4,128)(2,1)S(1)} %get-tuple-element.30, f32[64,4]{1,0:T(8,128)S(1)} %get-tuple-element.29), kind=kOutput, calls=%fused_computation.58 | convolution fusion | flops 33619968 | bytes 8717312 | tf_op jit(solution)/shard_map/bkgt,btkd->bkgd/dot_general | solution.py:55
  244.6 2.1 fusion.79
  249.3 55.1 %all-reduce.12.cloned.1.call-done = f32[64,5120]{1,0:T(8,128)} async-done(((f32[64,5120]{1,0:T(8,128)}), f32[64,5120]{1,0:T(8,128)}) %all-reduce.12.cloned.1.call-update) | async-done | bytes 1310736 | tf_op jit(solution)/shard_map/psum | solution.py:120
  304.4 1.7 fusion.25
  306.1 9.6 %fusion.8 = f32[64,1792]{1,0:T(8,128)S(1)} fusion(bf16[5120,1792]{1,0:T(8,128)(2,1)} %param.49, bf16[64,5120]{1,0:T(8,128)(2,1)S(1)} %get-tuple-element.4, f32[5120]{0:T(1024)S(1)} %convert_element_type.201, f32[64]{0:T(128)S(1)} %add_rsqrt_fusion.1), kind=kOutput, calls=%fused_computation.10 | convolution fusion | flops 1175945216 | bytes 19484928 | tf_op jit(solution)/shard_map/dot_general | solution.py:43
  315.7 18.7 %fusion.56 = f32[64,5120]{1,0:T(8,128)} fusion(bf16[1792,5120]{1,0:T(8,128)(2,1)} %param.51, bf16[5120,1792]{1,0:T(8,128)(2,1)} %param.50, f32[64,1792]{1,0:T(8,128)S(1)} %fusion.8, bf16[64,5120]{1,0:T(8,128)(2,1)S(1)} %get-tuple-element.4, f32[5120]{0:T(1024)S(1)} %convert_element_type.201, f32[64]{0:T(128)S(1)} %add_rsqrt_fusion.1), kind=kOutput, calls=%fused_computation.71 | convolution fusion | flops 2351038464 | bytes 39145728 | tf_op jit(solution)/shard_map/dot_general | solution.py:46
  334.5 57.6 %all-reduce.14.cloned.1.call-done = f32[64,5120]{1,0:T(8,128)} async-done(((f32[64,5120]{1,0:T(8,128)}), f32[64,5120]{1,0:T(8,128)}) %all-reduce.14.cloned.1.call-update) | async-done | bytes 1310736 | tf_op jit(solution)/shard_map/psum | solution.py:122
  392.1 2.5 fusion.28
  (73 shorter events, 10.6 us)
Async XLA Ops:
  7.2 3.3 copy-start
  7.2 69.3 %all-reduce.6.cloned.1.call-start = ((), (), s32[]{:S(2)}) async-start(), calls=%async_computation | async-start | bytes 262144 | tf_op jit(solution)/shard_map/psum | solution.py:63
  8.1 4.1 %copy-start.2 = (bf16[64,5120]{1,0:T(8,128)(2,1)S(1)}, bf16[64,5120]{1,0:T(8,128)(2,1)}, u32[]{:S(2)}) copy-start(bf16[64,5120]{1,0:T(8,128)(2,1)} %param.26) | copy-start | bytes 1966084
  8.1 4.1 %copy-start.11 = (bf16[5120,128]{1,0:T(8,128)(2,1)S(1)}, bf16[5120,128]{1,0:T(8,128)(2,1)}, u32[]{:S(2)}) copy-start(bf16[5120,128]{1,0:T(8,128)(2,1)} %param.37) | copy-start | bytes 3932164
  12.7 4.0 copy-start.4
  20.0 18.3 %copy-start.3 = (bf16[64,64,1,128]{3,1,2,0:T(8,128)(2,1)}, bf16[64,64,1,128]{3,1,2,0:T(8,128)(2,1)S(1)}, u32[]{:S(2)}) copy-start(bf16[64,64,1,128]{3,1,2,0:T(8,128)(2,1)S(1)} %get-tuple-element.15) | copy-start | bytes 3145732
  20.0 17.1 %copy-start.5 = (bf16[64,64,1,128]{3,1,2,0:T(8,128)(2,1)S(1)}, bf16[64,64,1,128]{3,1,2,0:T(8,128)(2,1)}, u32[]{:S(2)}) copy-start(bf16[64,64,1,128]{3,1,2,0:T(8,128)(2,1)} %get-tuple-element.16) | copy-start | bytes 3145732
  38.4 102.5 %all-reduce.8.cloned.1.call-start = ((), (), s32[]{:S(2)}) async-start(), calls=%async_computation.1 | async-start | bytes 2621440 | tf_op jit(solution)/shard_map/psum | solution.py:107
  82.1 0.7 copy-start.7
  82.2 146.3 %all-reduce.10.cloned.1.call-start = ((), (), s32[]{:S(2)}) async-start(), calls=%async_computation.2 | async-start | bytes 2621440 | tf_op jit(solution)/shard_map/psum | solution.py:109
  170.8 0.7 copy-start.8
  170.8 0.7 copy-start.12
  170.8 0.9 copy-start.6
  170.8 133.5 %all-reduce.12.cloned.1.call-start = ((), (), s32[]{:S(2)}) async-start(), calls=%async_computation.3 | async-start | bytes 2621440 | tf_op jit(solution)/shard_map/psum | solution.py:120
  233.9 10.7 %slice-start = ((s8[5242880]{0:T(1024)(128)(4,1)}), s8[1048576]{0:T(1024)(128)(4,1)S(1)}, s32[]{:S(2)}) async-start(s8[5242880]{0:T(1024)(128)(4,1)} %bitcast.71), calls=%async_computation.5 | async-start | bytes 2097152
  239.8 4.7 %slice-start.1 = ((s8[5242880]{0:T(1024)(128)(4,1)}), s8[4194304]{0:T(1024)(128)(4,1)S(1)}, s32[]{:S(2)}) async-start(s8[5242880]{0:T(1024)(128)(4,1)} %bitcast.71), calls=%async_computation.6 | async-start | bytes 8388608
  246.7 0.7 copy-start.13
  246.7 0.7 copy-start.9
  246.7 1.3 copy-start.10
  246.8 145.3 %all-reduce.14.cloned.1.call-start = ((), (), s32[]{:S(2)}) async-start(), calls=%async_computation.4 | async-start | bytes 2621440 | tf_op jit(solution)/shard_map/psum | solution.py:122
  392.1 2.5 copy-start.1
Sparse Core Ops, SparseCore 0:
  38.5 37.9 all-reduce.5
  82.3 58.5 all-reduce.7
  171.0 57.4 all-reduce.9
  246.9 57.4 all-reduce.11
  334.6 57.4 all-reduce.13
where the time goes:
time: 403 us; the launch traced here: 401 us
  waiting for transfers between devices  255 us (63%)
  matrix products  84.9 us (21%)
  blocking collectives  27.2 us (7%)
  other arithmetic  17.3 us (4%)
  between operations  14.1 us (3%)
    psum x1, waiting for transfers between devices, local_step(): lax.psum(jnp.dot(self_flat, self_wo, preferred_element_type=jnp.float32),...  58 us
    psum x1, waiting for transfers between devices, local_step(): lax.psum(mlp_partial(rms_norm(after_cross, cross_mlp_norm), cross_wgate,...  57.6 us
    psum x1, waiting for transfers between devices, local_step(): lax.psum(mlp_partial(rms_norm(after_attn, self_mlp_norm), self_wgate, sel...  56.7 us
    psum x1, waiting for transfers between devices, local_step(): lax.psum(jnp.dot(cross_flat, cross_wo, preferred_element_type=jnp.float32...  55.1 us
    dot_general x2, matrix products, mlp_partial(): return jnp.dot(hidden_act, w_down, preferred_element_type=jnp.float32)  37.4 us
    psum x1, waiting for transfers between devices, combine_sp(): total_out = lax.psum(part_out * factor[..., None], 'sp')  26.9 us
    dot_general x2, matrix products, mlp_partial(): jnp.dot(normed, w_gate, preferred_element_type=jnp.float32)  19.2 us
    pmax x1, blocking collectives, combine_sp(): glob_max = lax.pmax(part_max, 'sp')  16.1 us
  transfers between devices with their start and end apart: 5, of which 5 were waited for; matrix products, arithmetic and copies ran while one was open for 0% of the time, Pallas kernels for 0%

commit v1 on v0

v1 whole, which is shorter than its diff:
```python
import functools
import math
import jax
import jax.numpy as jnp
from jax import lax
from jax.experimental import pallas as pl
from jax.experimental.pallas import tpu as pltpu
from jax.sharding import PartitionSpec as P

NORM_EPS = 1e-5
ROPE_THETA = 500000.0
ROPE_FACTOR = 8.0
LOW_FREQ = 1.0
HIGH_FREQ = 4.0
ORIG_CTX = 8192.0
NEG_BIG = -1e30
MESH = pl.DeviceIdType.MESH
BF = jnp.bfloat16
F32 = jnp.float32
LANES = 128
GROUP_ROWS = 8
TILE_N = 256
PAIR_SLOTS = 5
NT_DIMS = (((1,), (1,)), ((), ()))
ORDER = ((2, 0), (2, 1), (1, 0), (1, 1), (3, 0), (3, 1), (0, 1), (0, 0))


def rope_freqs(head_dim):
    inv_freq = 1.0 / (ROPE_THETA ** (jnp.arange(0, head_dim, 2).astype(jnp.float32) / head_dim))
    wavelen = 2.0 * math.pi / inv_freq
    smooth = (ORIG_CTX / wavelen - LOW_FREQ) / (HIGH_FREQ - LOW_FREQ)
    mid_freq = (1.0 - smooth) * inv_freq / ROPE_FACTOR + smooth * inv_freq
    scaled = jnp.where(wavelen > ORIG_CTX / LOW_FREQ, inv_freq / ROPE_FACTOR, mid_freq)
    return jnp.where(wavelen < ORIG_CTX / HIGH_FREQ, inv_freq, scaled)


def self_kernel(pos_sm, hid_ref, g_ref, cos_ref, sin_ref, lpv_ref, wq_hbm, wk_hbm, wv_hbm, ks_hbm, vs_hbm,
                part_ref, ko_hbm, vo_hbm,
                xb, wq_b, wk_b, wv_b, kb, vb, q_s, kn_s, vn_s, w_sem, c_sem, o_sem, *, chunks, heads, scale):
    rows, hidden = hid_ref.shape
    hd = LANES
    tlen = kb.shape[0] // rows
    kc = hidden // chunks
    loads = []
    for i in range(chunks):
        sl = pl.ds(i * kc, kc)
        loads.append([pltpu.make_async_copy(wq_hbm.at[sl], wq_b.at[sl], w_sem.at[i, 0]),
                      pltpu.make_async_copy(wk_hbm.at[sl], wk_b.at[sl], w_sem.at[i, 1]),
                      pltpu.make_async_copy(wv_hbm.at[sl], wv_b.at[sl], w_sem.at[i, 2])])
        for cp in loads[-1]:
            cp.start()
    k_in = pltpu.make_async_copy(ks_hbm, kb, c_sem.at[0])
    v_in = pltpu.make_async_copy(vs_hbm, vb, c_sem.at[1])
    k_in.start()
    v_in.start()
    h32 = hid_ref[...].astype(F32)
    inv = lax.rsqrt(jnp.mean(h32 * h32, axis=-1, keepdims=True) + NORM_EPS)
    xb[...] = (h32 * inv * g_ref[...].astype(F32)).astype(BF)
    qa = ka = va = None
    for i in range(chunks):
        for cp in loads[i]:
            cp.wait()
        sl = pl.ds(i * kc, kc)
        xi = xb[:, i * kc:(i + 1) * kc]
        q_i = jnp.dot(xi, wq_b[sl], preferred_element_type=F32)
        k_i = jnp.dot(xi, wk_b[sl], preferred_element_type=F32)
        v_i = jnp.dot(xi, wv_b[sl], preferred_element_type=F32)
        qa, ka, va = (q_i, k_i, v_i) if i == 0 else (qa + q_i, ka + k_i, va + v_i)
    cos_t = cos_ref[...]
    sin_t = sin_ref[...]

    def rope(v):
        v = v.astype(BF).astype(F32)
        return (v * cos_t + pltpu.roll(v, hd // 2, 1) * sin_t).astype(BF).astype(F32)

    for h in range(heads):
        q_s[h] = rope(qa[:, h * hd:(h + 1) * hd])
    kn_s[...] = rope(ka)
    vn_s[...] = va.astype(BF).astype(F32)
    k_in.wait()
    v_in.wait()
    gr = GROUP_ROWS
    span = gr * tlen
    t_iota = lax.broadcasted_iota(jnp.int32, (tlen, hd), 0)
    col = lax.broadcasted_iota(jnp.int32, (heads * gr, span), 1)
    row = lax.broadcasted_iota(jnp.int32, (heads * gr, span), 0)
    same = (col // tlen) == (row % gr)
    tcol = col % tlen
    lane = lax.broadcasted_iota(jnp.int32, (gr, LANES), 1)

    def group(g, carry):
        base = pl.multiple_of(g * gr, gr)
        for i in range(gr):
            hit = t_iota == pos_sm[base + i]
            sl = pl.ds(pl.multiple_of((base + i) * tlen, tlen), tlen)
            kb[sl, :] = jnp.where(hit, kn_s[pl.ds(base + i, 1), :], kb[sl, :].astype(F32)).astype(BF)
            vb[sl, :] = jnp.where(hit, vn_s[pl.ds(base + i, 1), :], vb[sl, :].astype(F32)).astype(BF)
        gs = pl.ds(pl.multiple_of(g * span, span), span)
        rs = pl.ds(base, gr)
        qg = jnp.concatenate([q_s[h, rs, :] for h in range(heads)], axis=0).astype(BF)
        s = lax.dot_general(qg, kb[gs, :], NT_DIMS, preferred_element_type=F32) * scale
        lp = lpv_ref[rs, :]
        lp = jnp.concatenate([lp] * heads, axis=0)
        lp = jnp.concatenate([lp] * (span // LANES), axis=1)
        ok = jnp.logical_and(same, tcol <= lp)
        s = jnp.where(ok, s, NEG_BIG)
        m = jnp.max(s, axis=-1, keepdims=True)
        p = jnp.where(ok, jnp.exp(s - m), 0.0)
        l = jnp.sum(p, axis=-1, keepdims=True)
        o = jnp.dot(p.astype(BF), vb[gs, :], preferred_element_type=F32)
        stat = jnp.zeros((gr, LANES), F32)
        for h in range(heads):
            hs = slice(h * gr, (h + 1) * gr)
            part_ref[rs, h * hd:(h + 1) * hd] = o[hs]
            stat = jnp.where(lane == h, m[hs], stat)
            stat = jnp.where(lane == heads + h, l[hs], stat)
        part_ref[rs, heads * hd:] = stat
        return carry

    lax.fori_loop(0, rows // gr, group, 0)
    k_out = pltpu.make_async_copy(kb, ko_hbm, o_sem.at[0])
    v_out = pltpu.make_async_copy(vb, vo_hbm, o_sem.at[1])
    k_out.start()
    v_out.start()
    k_out.wait()
    v_out.wait()


def self_phase(pos, hid, gain, cos2, sin2, lpv, wq, wk, wv, ks, vs, *, scale):
    rows, hidden = hid.shape
    tlen = ks.shape[1]
    hd = ks.shape[2]
    heads = wq.shape[1] // hd
    chunks = 4
    ks = ks.reshape(rows * tlen, hd)
    vs = vs.reshape(rows * tlen, hd)
    vm = pl.BlockSpec(memory_space=pltpu.VMEM)
    anys = pl.BlockSpec(memory_space=pl.ANY)
    cache = jax.ShapeDtypeStruct(ks.shape, BF)
    part, ko, vo = pl.pallas_call(
        functools.partial(self_kernel, chunks=chunks, heads=heads, scale=scale),
        out_shape=(jax.ShapeDtypeStruct((rows, heads * hd + LANES), F32), cache, cache),
        in_specs=[pl.BlockSpec(memory_space=pltpu.SMEM)] + [vm] * 5 + [anys] * 5,
        out_specs=(vm, anys, anys),
        scratch_shapes=[
            pltpu.VMEM((rows, hidden), BF),
            pltpu.VMEM(wq.shape, BF), pltpu.VMEM(wk.shape, BF), pltpu.VMEM(wv.shape, BF),
            pltpu.VMEM(ks.shape, BF), pltpu.VMEM(vs.shape, BF),
            pltpu.VMEM((heads, rows, hd), F32), pltpu.VMEM((rows, hd), F32), pltpu.VMEM((rows, hd), F32),
            pltpu.SemaphoreType.DMA((chunks, 3)), pltpu.SemaphoreType.DMA((2,)), pltpu.SemaphoreType.DMA((2,)),
        ],
        compiler_params=pltpu.CompilerParams(vmem_limit_bytes=30 << 20),
        name="self_attention",
    )(pos, hid, gain, cos2, sin2, lpv, wq, wk, wv, ks, vs)
    return part, ko, vo


def step_kernel(part_ref, g2_ref, g3_ref, g4_ref, qn_ref, sc0_ref, sc1_ref, xv_ref,
                hid_hbm, wo_hbm, wg_hbm, wu_hbm, wd_hbm, wqc_hbm, woc_hbm, wgc_hbm, wuc_hbm, wdc_hbm, kc_hbm, vc_hbm,
                out_ref,
                wo_b, pair_b, down_b, kc_b, vc_b, hid_b, comb, sbuf, rbuf, piece, full, xb, act, ob, of, fin,
                wo_sem, pair_sem, down_sem, kv_sem, hid_sem, cs_sem, cr_sem, rs_ssem, rs_rsem, ag_ssem, ag_rsem,
                fd_ssem, fd_rsem, ff_ssem, ff_rsem, fc_ssem, fc_rsem, *, n_sp, n_tp, heads, scale):
    sp = lax.axis_index("sp")
    tp = lax.axis_index("tp")
    xx = tp // 2
    cc = tp % 2
    n_x = n_tp // 2
    rows = hid_b.shape[0]
    wide = hid_b.shape[1]
    hd = LANES
    gr = GROUP_ROWS
    r0 = pl.multiple_of(sp * rows, rows)
    n_pairs = wg_hbm.shape[1] // TILE_N

    def tp_at(k):
        dx, dc = ORDER[k]
        return ((xx + dx) % n_x) * 2 + (cc + dc) % 2

    def remote(src, dst, ssem, rsem, **dev):
        return pltpu.make_async_remote_copy(src_ref=src, dst_ref=dst, send_sem=ssem, recv_sem=rsem,
                                            device_id=dev, device_id_type=MESH)

    def pair_copies(p):
        slot = p % PAIR_SLOTS
        if p < n_pairs:
            a, b, c0 = wg_hbm, wu_hbm, (p * TILE_N, p * TILE_N)
        elif p == n_pairs:
            a, b, c0 = wqc_hbm, wqc_hbm, (0, TILE_N)
        else:
            q = p - n_pairs - 1
            a, b, c0 = wgc_hbm, wuc_hbm, (q * TILE_N, q * TILE_N)
        return [pltpu.make_async_copy(a.at[:, pl.ds(c0[0], TILE_N)], pair_b.at[slot, 0], pair_sem.at[slot, 0]),
                pltpu.make_async_copy(b.at[:, pl.ds(c0[1], TILE_N)], pair_b.at[slot, 1], pair_sem.at[slot, 1])]

    total_pairs = 2 * n_pairs + 1

    def start_pair(p):
        if p < total_pairs:
            for cp in pair_copies(p):
                cp.start()

    def down_copy(layer, k):
        src = (wd_hbm, wdc_hbm)[layer]
        return pltpu.make_async_copy(src.at[:, pl.ds(pl.multiple_of(tp_at(k) * wide, LANES), wide)],
                                     down_b.at[k], down_sem.at[k])

    wo_copy = pltpu.make_async_copy(wo_hbm, wo_b, wo_sem)
    woc_copy = pltpu.make_async_copy(woc_hbm, wo_b, wo_sem)
    hid_copy = pltpu.make_async_copy(
        hid_hbm.at[pl.ds(r0, rows), pl.ds(pl.multiple_of(tp * wide, LANES), wide)], hid_b, hid_sem)
    kc_copy = pltpu.make_async_copy(kc_hbm.at[pl.ds(r0, rows)], kc_b, kv_sem.at[0])
    vc_copy = pltpu.make_async_copy(vc_hbm.at[pl.ds(r0, rows)], vc_b, kv_sem.at[1])
    wo_copy.start()
    hid_copy.start()
    for p in range(PAIR_SLOTS):
        start_pair(p)
    for k in range(n_tp):
        down_copy(0, k).start()
    kc_copy.start()
    vc_copy.start()

    bar = pltpu.get_barrier_semaphore()
    for j in range(1, n_sp):
        pl.semaphore_signal(bar, inc=1, device_id={"sp": (sp + j) % n_sp}, device_id_type=MESH)
    for k in range(n_tp - 1):
        pl.semaphore_signal(bar, inc=1, device_id={"tp": tp_at(k)}, device_id_type=MESH)
    pl.semaphore_wait(bar, n_sp - 1 + n_tp - 1)

    sends = []
    for j in range(1, n_sp):
        peer = (sp + j) % n_sp
        cp = remote(part_ref.at[pl.ds(pl.multiple_of(peer * rows, rows), rows)], comb.at[j - 1],
                    cs_sem.at[j - 1], cr_sem.at[j - 1], sp=peer)
        cp.start()
        sends.append(cp)
    for cp in sends:
        cp.wait()
    own = part_ref[pl.ds(r0, rows), :]
    blocks = [own] + [comb[j] for j in range(n_sp - 1)]
    qw = heads * hd
    for h in range(heads):
        ms = [b[:, qw + h:qw + h + 1] for b in blocks]
        top = functools.reduce(jnp.maximum, ms)
        fs = [jnp.exp(m - top) for m in ms]
        den = sum(b[:, qw + heads + h:qw + heads + h + 1] * f for b, f in zip(blocks, fs))
        num = sum(b[:, h * hd:(h + 1) * hd] * f for b, f in zip(blocks, fs))
        ob[:, h * hd:(h + 1) * hd] = (num / den).astype(BF)

    def reduce_scatter(product):
        sent = []
        for k in range(n_tp - 1):
            sbuf[k] = product(k)
            cp = remote(sbuf.at[k], rbuf.at[k], rs_ssem.at[k], rs_rsem.at[k], tp=tp_at(k))
            cp.start()
            sent.append(cp)
        acc = product(n_tp - 1)
        for k in reversed(range(n_tp - 1)):
            sent[k].wait()
            acc = acc + rbuf[k]
        return acc

    def share(cur, slot):
        piece[slot] = cur
        full[tp] = cur
        sent = []
        for k in range(n_tp - 1):
            cp = remote(piece.at[slot], full.at[tp], ag_ssem.at[k], ag_rsem.at[k], tp=tp_at(k))
            cp.start()
            sent.append(cp)
        for cp in sent:
            cp.wait()

    def normed(g_ref):
        acc = jnp.zeros((rows, LANES), F32)
        for j in range(n_tp):
            v = full[j]
            v = v * v
            for i in range(wide // LANES):
                acc = acc + v[:, i * LANES:(i + 1) * LANES]
        inv = lax.rsqrt(jnp.sum(acc, axis=-1, keepdims=True) * (1.0 / (n_tp * wide)) + NORM_EPS)
        for j in range(n_tp):
            sl = slice(j * wide, (j + 1) * wide)
            xb[:, sl] = (full[j] * inv * g_ref[:, sl].astype(F32)).astype(BF)

    def gate_up(first):
        for t in range(n_pairs):
            p = first + t
            slot = p % PAIR_SLOTS
            for cp in pair_copies(p):
                cp.wait()
            gate = jnp.dot(xb[...], pair_b[slot, 0], preferred_element_type=F32).astype(BF).astype(F32)
            up = jnp.dot(xb[...], pair_b[slot, 1], preferred_element_type=F32).astype(BF).astype(F32)
            act[:, t * TILE_N:(t + 1) * TILE_N] = (gate * jax.nn.sigmoid(gate) * up).astype(BF)
            start_pair(p + PAIR_SLOTS)

    def down(layer):
        def product(k):
            down_copy(layer, k).wait()
            out = jnp.dot(act[...], down_b[k], preferred_element_type=F32)
            if layer == 0:
                down_copy(1, k).start()
            return out
        return reduce_scatter(product)

    def wo_product(k):
        return jnp.dot(ob[...], wo_b[:, pl.ds(pl.multiple_of(tp_at(k) * wide, LANES), wide)],
                       preferred_element_type=F32)

    def rounded(v):
        return v.astype(BF).astype(F32)

    wo_copy.wait()
    acc = reduce_scatter(wo_product)
    woc_copy.start()
    hid_copy.wait()
    share(rounded(hid_b[...].astype(F32) + acc), 0)
    normed(g2_ref)
    gate_up(0)
    acc = down(0)
    share(rounded(piece[0] + acc), 1)

    normed(g3_ref)
    p = n_pairs
    for cp in pair_copies(p):
        cp.wait()
    for i in range(2):
        qq = jnp.dot(xb[...], pair_b[p % PAIR_SLOTS, i], preferred_element_type=F32)
        for h in range(TILE_N // hd):
            v = rounded(qq[:, h * hd:(h + 1) * hd])
            inv = lax.rsqrt(jnp.mean(v * v, axis=-1, keepdims=True) + NORM_EPS)
            of[i * (TILE_N // hd) + h] = rounded(v * inv * qn_ref[...].astype(F32))
    start_pair(p + PAIR_SLOTS)
    kc_copy.wait()
    vc_copy.wait()
    n_vis = kc_b.shape[1]
    rmod = lax.broadcasted_iota(jnp.int32, (heads * gr, n_vis), 0) % gr
    for g in range(rows // gr):
        qg = jnp.concatenate([of[h, g * gr:(g + 1) * gr] for h in range(heads)], axis=0).astype(BF)
        s = jnp.zeros((heads * gr, n_vis), F32)
        for i in range(gr):
            s_i = lax.dot_general(qg, kc_b[g * gr + i], NT_DIMS, preferred_element_type=F32)
            s = jnp.where(rmod == i, s_i, s)
        valid = xv_ref[pl.ds(pl.multiple_of(r0 + g * gr, gr), gr), :]
        ok = jnp.concatenate([valid] * heads, axis=0) > 0
        s = jnp.where(ok, s * scale, NEG_BIG)
        m = jnp.max(s, axis=-1, keepdims=True)
        pr = jnp.where(ok, jnp.exp(s - m), 0.0)
        l = jnp.sum(pr, axis=-1, keepdims=True)
        o = jnp.zeros((heads * gr, hd), F32)
        for i in range(gr):
            o = o + jnp.dot(jnp.where(rmod == i, pr, 0.0).astype(BF), vc_b[g * gr + i], preferred_element_type=F32)
        o = o / l
        for h in range(heads):
            of[h, g * gr:(g + 1) * gr] = o[h * gr:(h + 1) * gr]
    for h in range(heads):
        ob[:, h * hd:(h + 1) * hd] = of[h].astype(BF)
    woc_copy.wait()
    acc = reduce_scatter(wo_product)
    s0 = sc0_ref[pl.ds(r0, rows), 0:1]
    share(rounded(piece[1] + s0 * acc), 0)

    normed(g4_ref)
    gate_up(n_pairs + 1)
    acc = down(1)
    s1 = sc1_ref[pl.ds(r0, rows), 0:1]
    fin[cc, sp, xx] = rounded(piece[0] + s1 * acc)

    half = rows // 2
    top = pl.ds(0, half)
    bot = pl.ds(half, half)

    def hop_x(src_sp, src_x, part, dx, ssem, rsem):
        blk = fin.at[cc, src_sp, src_x, part]
        return remote(blk, blk, ssem, rsem, tp=((xx + dx) % n_x) * 2 + cc)

    def hop_y(src_sp, src_x, part, dy, ssem, rsem):
        blk = fin.at[cc, src_sp, src_x, part]
        return remote(blk, blk, ssem, rsem, sp=(sp + dy) % n_sp)

    steps = (2, 1, 3)
    first = []
    for i, d in enumerate(steps):
        cx = hop_x(sp, xx, top, d, fd_ssem.at[0, i], fd_rsem.at[0, i])
        cy = hop_y(sp, xx, bot, d, fd_ssem.at[1, i], fd_rsem.at[1, i])
        cx.start()
        cy.start()
        first.append((cx, cy))
    second = []

    def forward(a, from_x, from_y):
        for i, d in enumerate(steps):
            cy = hop_y(sp, from_x, top, d, ff_ssem.at[0, a, i], ff_rsem.at[0, a, i])
            cx = hop_x(from_y, xx, bot, d, ff_ssem.at[1, a, i], ff_rsem.at[1, a, i])
            cy.start()
            cx.start()
            second.append((cx, cy))

    forward(0, xx, sp)
    for a, i in ((1, 1), (2, 2), (3, 0)):
        cx, cy = first[i]
        cx.wait()
        cy.wait()
        forward(a, (xx + n_x - steps[i]) % n_x, (sp + n_sp - steps[i]) % n_sp)
    for cx, cy in second:
        cx.wait()
        cy.wait()
    cp = remote(fin.at[cc], fin.at[cc], fc_ssem, fc_rsem, tp=xx * 2 + (1 - cc))
    cp.start()
    cp.wait()
    for c in range(2):
        for s in range(n_sp):
            for x in range(n_x):
                j = x * 2 + c
                out_ref[s * rows:(s + 1) * rows, j * wide:(j + 1) * wide] = fin[c, s, x].astype(BF)


def step_phase(part, gains, qnorm, sc0, sc1, xvalid, hid, weights, kc, vc, *, n_sp, n_tp, heads, scale):
    all_rows, hidden = hid.shape
    rows = all_rows // n_sp
    wide = hidden // n_tp
    mlp = weights[1].shape[1]
    n_vis, hd = kc.shape[1], kc.shape[2]
    vm = pl.BlockSpec(memory_space=pltpu.VMEM)
    anys = pl.BlockSpec(memory_space=pl.ANY)
    dma = pltpu.SemaphoreType.DMA
    n_x = n_tp // 2
    peers = n_tp - 1
    return pl.pallas_call(
        functools.partial(step_kernel, n_sp=n_sp, n_tp=n_tp, heads=heads, scale=scale),
        out_shape=jax.ShapeDtypeStruct((all_rows, hidden), BF),
        in_specs=[vm] * 8 + [anys] * 12,
        out_specs=vm,
        scratch_shapes=[
            pltpu.VMEM(weights[0].shape, BF),
            pltpu.VMEM((PAIR_SLOTS, 2, hidden, TILE_N), BF),
            pltpu.VMEM((n_tp, mlp, wide), BF),
            pltpu.VMEM((rows, n_vis, hd), BF), pltpu.VMEM((rows, n_vis, hd), BF),
            pltpu.VMEM((rows, wide), BF),
            pltpu.VMEM((n_sp - 1, rows, part.shape[1]), F32),
            pltpu.VMEM((peers, rows, wide), F32), pltpu.VMEM((peers, rows, wide), F32),
            pltpu.VMEM((2, rows, wide), F32),
            pltpu.VMEM((n_tp, rows, wide), F32),
            pltpu.VMEM((rows, hidden), BF),
            pltpu.VMEM((rows, mlp), BF),
            pltpu.VMEM((rows, heads * hd), BF),
            pltpu.VMEM((heads, rows, hd), F32),
            pltpu.VMEM((2, n_sp, n_x, rows, wide), F32),
            dma, dma((PAIR_SLOTS, 2)), dma((n_tp,)), dma((2,)), dma,
            dma((n_sp - 1,)), dma((n_sp - 1,)), dma((peers,)), dma((peers,)), dma((peers,)), dma((peers,)),
            dma((2, 3)), dma((2, 3)), dma((2, 4, 3)), dma((2, 4, 3)), dma, dma,
        ],
        compiler_params=pltpu.CompilerParams(collective_id=1, has_side_effects=True, vmem_limit_bytes=67043328),
        name="decode_step",
    )(part, *gains, qnorm, sc0, sc1, xvalid, hid, *weights, kc, vc)


def solution(mesh):
    cache_spec = P('dp', 'sp', 'tp', None)
    cross_spec = P('dp', None, 'tp', None)
    row_spec = P('dp', None)
    vec_spec = P('dp')
    full_spec = P(None)
    col_spec = P(None, 'tp')
    split_rows = P('tp', None)
    in_specs = (row_spec, vec_spec, cache_spec, cache_spec, cross_spec, cross_spec, row_spec, vec_spec,
                full_spec, col_spec, col_spec, col_spec, split_rows, full_spec, col_spec, col_spec, split_rows,
                full_spec, col_spec, full_spec, split_rows, full_spec, full_spec, col_spec, col_spec, split_rows)
    out_specs = (row_spec, cache_spec, cache_spec)
    n_sp = mesh.shape['sp']
    n_tp = mesh.shape['tp']

    def local_step(hidden, new_pos, k_self, v_self, k_cross, v_cross, xvalid, rowmask,
                   self_attn_norm, self_wq, self_wk, self_wv, self_wo, self_mlp_norm,
                   self_wgate, self_wup, self_wdown, cross_attn_norm, cross_wq, cross_qnorm,
                   cross_wo, cross_gates, cross_mlp_norm, cross_wgate, cross_wup, cross_wdown):
        batch_rows = hidden.shape[0]
        len_local = k_self.shape[1]
        head_dim = k_self.shape[3]
        heads = self_wq.shape[1] // head_dim
        scale = head_dim ** -0.5
        angles = new_pos.astype(F32)[:, None] * rope_freqs(head_dim)[None, :]
        cos_t = jnp.cos(angles)
        sin_t = jnp.sin(angles)
        cos2 = jnp.concatenate([cos_t, cos_t], axis=-1)
        sin2 = jnp.concatenate([-sin_t, sin_t], axis=-1)
        local_pos = new_pos - lax.axis_index('sp') * len_local
        lpv = jnp.broadcast_to(local_pos[:, None], (batch_rows, LANES))
        flat = (batch_rows, len_local, head_dim)
        part, ko, vo = self_phase(local_pos, hidden, self_attn_norm[None, :], cos2, sin2, lpv, self_wq, self_wk, self_wv,
                                  k_self.reshape(flat), v_self.reshape(flat), scale=scale)
        gate_vals = jnp.tanh(cross_gates.astype(F32))
        row_scale = jnp.broadcast_to(rowmask.astype(F32)[:, None], (batch_rows, LANES))
        gains = (self_mlp_norm[None, :], cross_attn_norm[None, :], cross_mlp_norm[None, :])
        weights = (self_wo, self_wgate, self_wup, self_wdown, cross_wq, cross_wo, cross_wgate, cross_wup, cross_wdown)
        cflat = (batch_rows, k_cross.shape[1], head_dim)
        h4 = step_phase(part, gains, cross_qnorm[None, :], gate_vals[0] * row_scale, gate_vals[1] * row_scale, xvalid,
                        hidden, weights, k_cross.reshape(cflat), v_cross.reshape(cflat),
                        n_sp=n_sp, n_tp=n_tp, heads=heads, scale=scale)
        return h4, ko.reshape(k_self.shape), vo.reshape(v_self.shape)

    return jax.shard_map(local_step, mesh=mesh, in_specs=in_specs, out_specs=out_specs, check_vma=False)
```

time: 403 us -> 122 us (0.30)
  waiting for transfers between devices: 255 us -> 0 us
  Pallas kernels: 0 us -> 98.6 us
  matrix products: 84.9 us -> 0 us
  blocking collectives: 27.2 us -> 0 us
  local copies, waits for them, and re-layouts: 2.01 us -> 18.6 us
  other arithmetic: 17.3 us -> 2.98 us
  between operations: 14.1 us -> 0.7 us
    psum x5 -> x0, waiting for transfers between devices: 254 us -> none  [the longest x1 58 us: local_step(): lax.psum(jnp.dot(self_flat, self_wo, preferred_element_type=jnp.float32),...]
    pallas_call x0 -> x2, Pallas kernels: none -> 98.6 us  [the longest x1 90.1 us: step_phase(): pl.pallas_call(functools.partial(step_kernel, n_sp=n_sp, n_tp=n_tp, heads...]
    dot_general x13 -> x0, matrix products: 79 us -> none  [the longest x2 37.4 us: mlp_partial(): return jnp.dot(hidden_act, w_down, preferred_element_type=jnp.float32)]
    pmax x1 -> x0, blocking collectives: 16.1 us -> none  [combine_sp(): glob_max = lax.pmax(part_max, 'sp')]
    psum x1 -> x0, blocking collectives: 11.1 us -> none  [combine_sp(): total_sum = lax.psum(part_sum * factor, 'sp')]
    unnamed x32 -> x15, local copies, waits for them, and re-layouts: 1.33 us -> 11.3 us
    reduce_sum x6 -> x0, other arithmetic: 6.76 us -> none  [the longest x5 6.52 us: rms_norm(): jnp.mean(vals32 * vals32, axis=-1, keepdims=True) + NORM_EPS]
    broadcast_in_dim x0 -> x7, local copies, waits for them, and re-layouts: none -> 6.13 us  [the longest x2 1.37 us: local_step(): jnp.broadcast_to(rowmask.astype(F32)[:, None], (batch_rows, LANES))]
  transfers between devices with their start and end apart: 5 -> 0, of which waited for: 5 -> 0; matrix products, arithmetic and copies ran while one was open for 0% -> 0% of each run, Pallas kernels for 0% -> 0%
where the time goes in v1:
time: 122 us; the launch traced here: 121 us
  Pallas kernels  98.6 us (81%)
  local copies, waits for them, and re-layouts  18.6 us (15%)
  other arithmetic  2.98 us (2%)
    pallas_call x1, Pallas kernels, step_phase(): pl.pallas_call(functools.partial(step_kernel, n_sp=n_sp, n_tp=n_tp, heads...  90.1 us
    unnamed x15, local copies, waits for them, and re-layouts  11.3 us
    pallas_call x1, Pallas kernels, self_phase(): pl.pallas_call(functools.partial(self_kernel, chunks=chunks, heads=heads,...  8.58 us

profile of v1, /device:TPU:97, one launch (start us, length us, event | category | flops | bytes accessed | tf_op | source)
XLA Modules:
  0.0 121.0 jit_solution(5732683370518751856)
XLA Ops:
  0.6 0.7 tanh.3
  1.3 0.6 fusion.1
  1.9 2.0 %convert_multiply_fusion = (f32[64]{0:T(128)S(1)}, f32[64]{0:T(128)S(1)}) fusion(s32[64]{0:T(128)} %param.33, f32[]{:T(128)} %bitcast.4, f32[]{:T(128)} %bitcast.3), kind=kLoop, calls=%fused_computation.7 | loop fusion | flops 192 | bytes 776 | tf_op jit(solution)/shard_map/mul | solution.py:497
  3.9 0.7 fusion.2
  4.6 0.7 broadcast_in_dim.31.g_ref
  5.3 1.3 %broadcast_in_dim.33.g2_ref = bf16[1,5120]{1,0:T(2,128)(2,1)} reshape(bf16[5120]{0:T(1024)(128)(2,1)} %param.39) | data formatting | bytes 20480 | tf_op jit(solution)/shard_map/broadcast_in_dim | solution.py:494
  6.6 1.3 %broadcast_in_dim.34.g3_ref = bf16[1,5120]{1,0:T(2,128)(2,1)} reshape(bf16[5120]{0:T(1024)(128)(2,1)} %param.43) | data formatting | bytes 20480 | tf_op jit(solution)/shard_map/broadcast_in_dim | solution.py:494
  7.9 1.3 %broadcast_in_dim.35.g4_ref = bf16[1,5120]{1,0:T(2,128)(2,1)} reshape(bf16[5120]{0:T(1024)(128)(2,1)} %param.48) | data formatting | bytes 20480 | tf_op jit(solution)/shard_map/broadcast_in_dim | solution.py:494
  9.3 0.7 broadcast_in_dim.38.sc1_ref
  10.0 0.1 broadcast_in_dim.32.lpv_ref
  10.0 0.7 broadcast_in_dim.37.sc0_ref
  10.7 0.2 fusion
  10.9 0.1 pad_maximum_fusion
  11.0 2.5 %copy-done = bf16[5120,512]{1,0:T(8,128)(2,1)S(1)} copy-done((bf16[5120,512]{1,0:T(8,128)(2,1)S(1)}, bf16[5120,512]{1,0:T(8,128)(2,1)}, u32[]{:S(2)}) %copy-start) | copy-done | bytes 5242904
  13.5 1.1 copy-done.1
  14.6 1.3 %copy-done.2 = bf16[5120,128]{1,0:T(8,128)(2,1)S(1)} copy-done((bf16[5120,128]{1,0:T(8,128)(2,1)S(1)}, bf16[5120,128]{1,0:T(8,128)(2,1)}, u32[]{:S(2)}) %copy-start.2) | copy-done | bytes 1310744
  15.9 1.3 %copy-done.3 = bf16[5120,128]{1,0:T(8,128)(2,1)S(1)} copy-done((bf16[5120,128]{1,0:T(8,128)(2,1)S(1)}, bf16[5120,128]{1,0:T(8,128)(2,1)}, u32[]{:S(2)}) %copy-start.3) | copy-done | bytes 1310744
  17.2 1.2 %copy-done.4 = bf16[64,64,1,128]{3,1,2,0:T(8,128)(2,1)S(1)} copy-done((bf16[64,64,1,128]{3,1,2,0:T(8,128)(2,1)S(1)}, bf16[64,64,1,128]{3,1,2,0:T(8,128)(2,1)}, u32[]{:S(2)}) %copy-start.4) | copy-done | bytes 1048600
  18.5 1.2 %copy-done.5 = bf16[64,64,1,128]{3,1,2,0:T(8,128)(2,1)S(1)} copy-done((bf16[64,64,1,128]{3,1,2,0:T(8,128)(2,1)S(1)}, bf16[64,64,1,128]{3,1,2,0:T(8,128)(2,1)}, u32[]{:S(2)}) %copy-start.5) | copy-done | bytes 1048600
  19.7 8.6 %self_attention.1 = (f32[64,640]{1,0:T(8,128)S(1)}, bf16[4096,128]{1,0:T(8,128)(2,1)}, bf16[4096,128]{1,0:T(8,128)(2,1)}) custom-call(s32[64]{0:T(128)S(1)} %get-tuple-element.20.pos_sm, bf16[64,5120]{1,0:T(8,128)(2,1)S(1)} %copy-done.1, bf16[1,5120]{1,0:T(2,128)(2,1)S(1)} %broadcast_in_dim.31.g_ref, f32[64,128]{1,0:T(8,128)S(1)} %get-tuple-element.21.cos_ref, ...), custom_call_target="tpu_custom_call" | custom-call | tf_op jit(solution)/shard_map/self_attention/pallas_call | solution.py:140
  28.3 0.0 copy-start.6
  28.3 0.7 copy-done.6
  28.9 90.1 %decode_step.1 = bf16[64,5120]{1,0:T(8,128)(2,1)} custom-call(f32[64,640]{1,0:T(8,128)} %copy-done.6, bf16[1,5120]{1,0:T(2,128)(2,1)} %broadcast_in_dim.33.g2_ref, bf16[1,5120]{1,0:T(2,128)(2,1)} %broadcast_in_dim.34.g3_ref, bf16[1,5120]{1,0:T(2,128)(2,1)} %broadcast_in_dim.35.g4_ref, bf16[1,128]{1,0:T(2,128)(2,1)} %bitcast.17, ...), custom_call_target="tpu_custom_call" | custom-call | tf_op jit(solution)/shard_map/decode_step/pallas_call | solution.py:429
  119.0 2.0 %copy.32 = bf16[64,5120]{1,0:T(8,128)(2,1)} copy(bf16[64,5120]{1,0:T(8,128)(2,1)} %decode_step.1) | data formatting | bytes 1310720
  (7 shorter events, 0.0 us)
Async XLA Ops:
  11.0 2.5 %copy-start = (bf16[5120,512]{1,0:T(8,128)(2,1)S(1)}, bf16[5120,512]{1,0:T(8,128)(2,1)}, u32[]{:S(2)}) copy-start(bf16[5120,512]{1,0:T(8,128)(2,1)} %wq_hbm.1) | copy-start | bytes 15728644
  13.5 1.1 copy-start.1
  14.6 1.3 %copy-start.2 = (bf16[5120,128]{1,0:T(8,128)(2,1)S(1)}, bf16[5120,128]{1,0:T(8,128)(2,1)}, u32[]{:S(2)}) copy-start(bf16[5120,128]{1,0:T(8,128)(2,1)} %wk_hbm.1) | copy-start | bytes 3932164
  15.9 1.3 %copy-start.3 = (bf16[5120,128]{1,0:T(8,128)(2,1)S(1)}, bf16[5120,128]{1,0:T(8,128)(2,1)}, u32[]{:S(2)}) copy-start(bf16[5120,128]{1,0:T(8,128)(2,1)} %wv_hbm.1) | copy-start | bytes 3932164
  17.2 1.2 %copy-start.4 = (bf16[64,64,1,128]{3,1,2,0:T(8,128)(2,1)S(1)}, bf16[64,64,1,128]{3,1,2,0:T(8,128)(2,1)}, u32[]{:S(2)}) copy-start(bf16[64,64,1,128]{3,1,2,0:T(8,128)(2,1)} %param.28) | copy-start | bytes 3145732
  18.4 1.2 %copy-start.5 = (bf16[64,64,1,128]{3,1,2,0:T(8,128)(2,1)S(1)}, bf16[64,64,1,128]{3,1,2,0:T(8,128)(2,1)}, u32[]{:S(2)}) copy-start(bf16[64,64,1,128]{3,1,2,0:T(8,128)(2,1)} %param.29) | copy-start | bytes 3145732
  28.3 0.7 copy-start.6

commit v2 on v1

v2 whole, which is shorter than its diff:
```python
import functools
import math
import jax
import jax.numpy as jnp
import numpy as np
from jax import lax
from jax.experimental import pallas as pl
from jax.experimental.pallas import tpu as pltpu
from jax.sharding import PartitionSpec as P

NORM_EPS = 1e-5
ROPE_THETA = 500000.0
ROPE_FACTOR = 8.0
LOW_FREQ = 1.0
HIGH_FREQ = 4.0
ORIG_CTX = 8192.0
NEG_BIG = -1e30
MESH = pl.DeviceIdType.MESH
BF = jnp.bfloat16
F32 = jnp.float32
LANES = 128
GROUP_ROWS = 8
CHUNK_SLOTS = 5
NT_DIMS = (((1,), (1,)), ((), ()))
ORDER = ((0, 0), (0, 1), (1, 0), (3, 0), (1, 1), (3, 1), (2, 0), (2, 1))
FROM = (0, 1, 3, 2, 5, 4, 6, 7)
CHIPS = (2, 1, 3, 0)


def rope_table(head_dim):
    inv_freq = (1.0 / (ROPE_THETA ** (np.arange(0, head_dim, 2) / head_dim))).astype(np.float32)
    wavelen = 2.0 * math.pi / inv_freq
    smooth = (ORIG_CTX / wavelen - LOW_FREQ) / (HIGH_FREQ - LOW_FREQ)
    mid_freq = (1.0 - smooth) * inv_freq / ROPE_FACTOR + smooth * inv_freq
    scaled = np.where(wavelen > ORIG_CTX / LOW_FREQ, inv_freq / ROPE_FACTOR, mid_freq)
    freqs = np.where(wavelen < ORIG_CTX / HIGH_FREQ, inv_freq, scaled)
    table = np.zeros((8, head_dim), np.float32)
    table[0] = np.concatenate([freqs, freqs])
    table[1] = np.where(np.arange(head_dim) < head_dim // 2, -1.0, 1.0)
    return jnp.asarray(table)


def self_kernel(pos_sm, freq_hbm, hid_hbm, g_hbm, wq_hbm, wk_hbm, wv_hbm, ks_hbm, vs_hbm,
                part_hbm, ko_hbm, vo_hbm,
                freq_b, hid_b, g_b, xb, w_b, wk_b, wv_b, kb, vb, q_s, kn_s, vn_s, lp_s, s_s, part_b,
                i_sem, w_sem, c_sem, o_sem, *, chunks, heads, scale):
    rows, hidden = hid_b.shape
    hd = LANES
    tlen = kb.shape[0] // rows
    kc = hidden // chunks
    qw = heads * hd
    small = [pltpu.make_async_copy(hid_hbm, hid_b, i_sem.at[0]), pltpu.make_async_copy(g_hbm, g_b, i_sem.at[1]),
             pltpu.make_async_copy(freq_hbm, freq_b, i_sem.at[2])]
    for cp in small:
        cp.start()
    kv_in = [pltpu.make_async_copy(wk_hbm, wk_b, i_sem.at[3]), pltpu.make_async_copy(wv_hbm, wv_b, i_sem.at[4]),
             pltpu.make_async_copy(ks_hbm, kb, c_sem.at[0]), pltpu.make_async_copy(vs_hbm, vb, c_sem.at[1])]
    for cp in kv_in:
        cp.start()
    loads = []
    for i in range(chunks):
        sl = pl.ds(i * kc, kc)
        loads.append(pltpu.make_async_copy(wq_hbm.at[sl], w_b.at[sl], w_sem.at[i]))
        loads[-1].start()
    for cp in small:
        cp.wait()
    acc = jnp.zeros((rows, LANES), F32)
    for c in range(hidden // LANES):
        v = hid_b[:, c * LANES:(c + 1) * LANES].astype(F32)
        acc = acc + v * v
    inv = lax.rsqrt(jnp.sum(acc, axis=-1, keepdims=True) * (1.0 / hidden) + NORM_EPS)
    g_all = g_b[...].astype(F32)
    for c in range(hidden // LANES):
        sl = slice(c * LANES, (c + 1) * LANES)
        xb[:, sl] = (hid_b[:, sl].astype(F32) * inv * g_all[c:c + 1, :]).astype(BF)
    gr = GROUP_ROWS
    sub = lax.broadcasted_iota(jnp.int32, (gr, LANES), 0)
    pos_rows = []
    for g in range(rows // gr):
        pg = jnp.zeros((gr, LANES), jnp.int32)
        for i in range(gr):
            pg = jnp.where(sub == i, pos_sm[g * gr + i], pg)
        pos_rows.append(pg)
    pos_v = jnp.concatenate(pos_rows, axis=0)
    first = lax.axis_index("sp") * tlen
    lp_s[...] = pos_v - first
    ang = pos_v.astype(F32) * freq_b[0:1, :]
    cos_t = jnp.cos(ang)
    sin_t = jnp.sin(ang) * freq_b[1:2, :]

    def rope(v):
        v = v.astype(BF).astype(F32)
        return (v * cos_t + pltpu.roll(v, hd // 2, 1) * sin_t).astype(BF).astype(F32)

    for cp in kv_in:
        cp.wait()
    kn_s[...] = rope(jnp.dot(xb[...], wk_b[...], preferred_element_type=F32))
    vn_s[...] = jnp.dot(xb[...], wv_b[...], preferred_element_type=F32).astype(BF).astype(F32)
    span = gr * tlen
    t_iota = lax.broadcasted_iota(jnp.int32, (tlen, hd), 0)

    def update(g, carry):
        base = pl.multiple_of(g * gr, gr)
        for i in range(gr):
            hit = t_iota == pos_sm[base + i] - first
            sl = pl.ds(pl.multiple_of((base + i) * tlen, tlen), tlen)
            kb[sl, :] = jnp.where(hit, kn_s[pl.ds(base + i, 1), :], kb[sl, :].astype(F32)).astype(BF)
            vb[sl, :] = jnp.where(hit, vn_s[pl.ds(base + i, 1), :], vb[sl, :].astype(F32)).astype(BF)
        return carry

    lax.fori_loop(0, rows // gr, update, 0)
    k_out = pltpu.make_async_copy(kb, ko_hbm, o_sem.at[0])
    v_out = pltpu.make_async_copy(vb, vo_hbm, o_sem.at[1])
    k_out.start()
    v_out.start()
    qq = None
    for i in range(chunks):
        loads[i].wait()
        part = jnp.dot(xb[:, i * kc:(i + 1) * kc], w_b[i * kc:(i + 1) * kc, :], preferred_element_type=F32)
        qq = part if qq is None else qq + part
    for h in range(heads):
        q_s[h] = rope(qq[:, h * hd:(h + 1) * hd])
    groups = rows // gr
    for g in range(groups):
        rs = slice(g * gr, (g + 1) * gr)
        qg = jnp.concatenate([q_s[h, rs, :] for h in range(heads)], axis=0).astype(BF)
        s_s[g] = lax.dot_general(qg, kb[g * span:(g + 1) * span, :], NT_DIMS, preferred_element_type=F32)
    col = lax.broadcasted_iota(jnp.int32, (heads * gr, LANES), 1)
    row = lax.broadcasted_iota(jnp.int32, (heads * gr, LANES), 0)
    lane = lax.broadcasted_iota(jnp.int32, (gr, LANES), 1)
    tcol = col % tlen
    for g in range(groups):
        rs = slice(g * gr, (g + 1) * gr)
        lp = jnp.concatenate([lp_s[rs, :]] * heads, axis=0)
        seen = tcol <= lp
        oks, ss = [], []
        for c in range(span // LANES):
            ok = jnp.logical_and(seen, c * (LANES // tlen) + col // tlen == row % gr)
            oks.append(ok)
            ss.append(jnp.where(ok, s_s[g, :, c * LANES:(c + 1) * LANES] * scale, NEG_BIG))
        m = jnp.max(functools.reduce(jnp.maximum, ss), axis=-1, keepdims=True)
        ps = [jnp.where(ok, jnp.exp(s - m), 0.0) for ok, s in zip(oks, ss)]
        l = jnp.sum(functools.reduce(jnp.add, ps), axis=-1, keepdims=True)
        p = jnp.concatenate(ps, axis=1).astype(BF)
        o = jnp.dot(p, vb[g * span:(g + 1) * span, :], preferred_element_type=F32)
        stat = jnp.zeros((gr, LANES), F32)
        for h in range(heads):
            hs = slice(h * gr, (h + 1) * gr)
            part_b[rs, h * hd:(h + 1) * hd] = o[hs]
            stat = jnp.where(lane == h, m[hs], stat)
            stat = jnp.where(lane == heads + h, l[hs], stat)
        part_b[rs, qw:] = stat
    p_out = pltpu.make_async_copy(part_b, part_hbm, o_sem.at[2])
    p_out.start()
    p_out.wait()
    k_out.wait()
    v_out.wait()


def self_phase(pos, hid, gain, wq, wk, wv, ks, vs, *, scale):
    rows, hidden = hid.shape
    tlen = ks.shape[1]
    hd = ks.shape[2]
    heads = wq.shape[1] // hd
    chunks = 4
    ks = ks.reshape(rows * tlen, hd)
    vs = vs.reshape(rows * tlen, hd)
    freq = rope_table(hd)
    anys = pl.BlockSpec(memory_space=pl.ANY)
    cache = jax.ShapeDtypeStruct(ks.shape, BF)
    pshape = (rows, heads * hd + LANES)
    return pl.pallas_call(
        functools.partial(self_kernel, chunks=chunks, heads=heads, scale=scale),
        out_shape=(jax.ShapeDtypeStruct(pshape, F32), cache, cache),
        in_specs=[pl.BlockSpec(memory_space=pltpu.SMEM)] + [anys] * 8,
        out_specs=(anys, anys, anys),
        scratch_shapes=[
            pltpu.VMEM(freq.shape, F32), pltpu.VMEM((rows, hidden), BF), pltpu.VMEM(gain.shape, BF),
            pltpu.VMEM((rows, hidden), BF), pltpu.VMEM(wq.shape, BF),
            pltpu.VMEM(wk.shape, BF), pltpu.VMEM(wv.shape, BF),
            pltpu.VMEM(ks.shape, BF), pltpu.VMEM(vs.shape, BF),
            pltpu.VMEM((heads, rows, hd), F32), pltpu.VMEM((rows, hd), F32), pltpu.VMEM((rows, hd), F32),
            pltpu.VMEM((rows, LANES), jnp.int32),
            pltpu.VMEM((rows // GROUP_ROWS, heads * GROUP_ROWS, GROUP_ROWS * tlen), F32), pltpu.VMEM(pshape, F32),
            pltpu.SemaphoreType.DMA((5,)), pltpu.SemaphoreType.DMA((chunks,)), pltpu.SemaphoreType.DMA((2,)),
            pltpu.SemaphoreType.DMA((3,)),
        ],
        compiler_params=pltpu.CompilerParams(vmem_limit_bytes=60 << 20),
        name="self_attention",
    )(pos, freq, hid, gain, wq, wk, wv, ks, vs)


def step_kernel(mask_sm, gate_sm, part_hbm, g2_hbm, g3_hbm, g4_hbm, qn_hbm, xv_hbm,
                hid_hbm, wo_hbm, wg_hbm, wu_hbm, wd_hbm, wqc_hbm, woc_hbm, wgc_hbm, wuc_hbm, wdc_hbm, kc_hbm, vc_hbm,
                out_ref,
                wo_b, chunk_b, qc_b, down_b, kc_b, vc_b, hid_b, comb, sbuf, rbuf, piece, full, stat, stats, acc_s, act, ob, of,
                fin, part_ref, gain_b, gain_f, qn_ref, xv_ref, small_sem,
                wo_sem, chunk_sem, qc_sem, down_sem, kv_sem, hid_sem, cs_sem, cr_sem, rs_ssem, rs_rsem, ag_ssem, ag_rsem,
                st_ssem, st_rsem, fd_ssem, fd_rsem, ff_ssem, ff_rsem, fc_ssem, fc_rsem, *, n_sp, n_tp, heads, scale):
    sp = lax.axis_index("sp")
    tp = lax.axis_index("tp")
    xx = tp // 2
    cc = tp % 2
    n_x = n_tp // 2
    rows = hid_b.shape[0]
    wide = hid_b.shape[1]
    mlp = act.shape[1]
    hd = LANES
    gr = GROUP_ROWS
    per = wide // LANES
    r0 = pl.multiple_of(sp * rows, rows)

    def tp_at(k):
        dx, dc = ORDER[k]
        return ((xx + dx) % n_x) * 2 + (cc + dc) % 2

    def remote(src, dst, ssem, rsem, **dev):
        return pltpu.make_async_remote_copy(src_ref=src, dst_ref=dst, send_sem=ssem, recv_sem=rsem,
                                            device_id=dev, device_id_type=MESH)

    def chunk_copies(n):
        slot = n % CHUNK_SLOTS
        a, b = ((wg_hbm, wu_hbm), (wgc_hbm, wuc_hbm))[n // n_tp]
        src = pl.ds(pl.multiple_of(tp_at(n % n_tp) * wide, wide), wide)
        return [pltpu.make_async_copy(a.at[src], chunk_b.at[slot, :, pl.ds(0, mlp)], chunk_sem.at[slot, 0]),
                pltpu.make_async_copy(b.at[src], chunk_b.at[slot, :, pl.ds(mlp, mlp)], chunk_sem.at[slot, 1])]

    def start_chunks(first, last):
        for n in range(first, last):
            for cp in chunk_copies(n):
                cp.start()

    def chip_at(i):
        return (xx + CHIPS[i]) % n_x

    def down_copy(layer, i):
        src = (wd_hbm, wdc_hbm)[layer]
        return pltpu.make_async_copy(src.at[:, pl.ds(pl.multiple_of(chip_at(i) * 2 * wide, LANES), 2 * wide)],
                                     down_b.at[i], down_sem.at[i])

    wo_copy = pltpu.make_async_copy(wo_hbm, wo_b, wo_sem)
    woc_copy = pltpu.make_async_copy(woc_hbm, wo_b, wo_sem)
    qc_copy = pltpu.make_async_copy(wqc_hbm, qc_b, qc_sem)
    hid_copy = pltpu.make_async_copy(
        hid_hbm.at[pl.ds(r0, rows), pl.ds(pl.multiple_of(tp * wide, LANES), wide)], hid_b, hid_sem)
    kc_copy = pltpu.make_async_copy(kc_hbm.at[pl.ds(r0, rows)], kc_b, kv_sem.at[0])
    vc_copy = pltpu.make_async_copy(vc_hbm.at[pl.ds(r0, rows)], vc_b, kv_sem.at[1])
    small = [pltpu.make_async_copy(part_hbm, part_ref, small_sem.at[0]),
             pltpu.make_async_copy(g2_hbm, gain_b.at[0], small_sem.at[1]),
             pltpu.make_async_copy(g3_hbm, gain_b.at[1], small_sem.at[2]),
             pltpu.make_async_copy(g4_hbm, gain_b.at[2], small_sem.at[3]),
             pltpu.make_async_copy(qn_hbm, qn_ref, small_sem.at[4]),
             pltpu.make_async_copy(xv_hbm.at[pl.ds(r0, rows)], xv_ref, small_sem.at[5])]
    for cp in small:
        cp.start()

    bar = pltpu.get_barrier_semaphore()
    for j in range(1, n_sp):
        pl.semaphore_signal(bar, inc=1, device_id={"sp": (sp + j) % n_sp}, device_id_type=MESH)
    for k in range(1, n_tp):
        pl.semaphore_signal(bar, inc=1, device_id={"tp": tp_at(k)}, device_id_type=MESH)

    wo_copy.start()
    hid_copy.start()
    start_chunks(0, 3)
    for cp in small:
        cp.wait()
    for i in range(3):
        g_all = gain_b[i].astype(F32)
        for j in range(n_tp):
            gain_f[i, j] = g_all[j * per:(j + 1) * per, :]
    pl.semaphore_wait(bar, n_sp - 1 + n_tp - 1)

    sends = []
    for i, j in enumerate((2, 1, 3)):
        peer = (sp + j) % n_sp
        cp = remote(part_ref.at[pl.ds(pl.multiple_of(peer * rows, rows), rows)], comb.at[i],
                    cs_sem.at[i], cr_sem.at[i], sp=peer)
        cp.start()
        sends.append(cp)
    start_chunks(3, CHUNK_SLOTS)
    for cp in sends:
        cp.wait()
    own = part_ref[pl.ds(r0, rows), :]
    blocks = [own] + [comb[j] for j in range(n_sp - 1)]
    qw = heads * hd
    for h in range(heads):
        ms = [b[:, qw + h:qw + h + 1] for b in blocks]
        top = functools.reduce(jnp.maximum, ms)
        fs = [jnp.exp(m - top) for m in ms]
        den = sum(b[:, qw + heads + h:qw + heads + h + 1] * f for b, f in zip(blocks, fs))
        num = sum(b[:, h * hd:(h + 1) * hd] * f for b, f in zip(blocks, fs))
        ob[:, h * hd:(h + 1) * hd] = (num / den).astype(BF)

    def reduce_scatter(product, then=None):
        sent = []
        for i in range(n_x):
            out = product(i)
            sbuf[2 * i] = out[:, :wide]
            sbuf[2 * i + 1] = out[:, wide:]
            if i < n_x - 1:
                for c in range(2):
                    cp = remote(sbuf.at[2 * i + c], rbuf.at[2 * i + cc], rs_ssem.at[2 * i + c], rs_rsem.at[2 * i + cc],
                                tp=chip_at(i) * 2 + c)
                    cp.start()
                    sent.append(cp)
        last = 2 * (n_x - 1)
        cp = remote(sbuf.at[last + 1 - cc], rbuf.at[last], rs_ssem.at[last], rs_rsem.at[last], tp=xx * 2 + 1 - cc)
        cp.start()
        sent.append(cp)
        if then is not None:
            then()
        acc = sbuf[last + cc]
        for j in (6, 2, 3, 4, 5, 0, 1):
            remote(sbuf.at[j], rbuf.at[j], rs_ssem.at[j], rs_rsem.at[j], tp=xx * 2 + 1 - cc).wait_recv()
            acc = acc + rbuf[j]
        for cp in sent:
            cp.wait_send()
        return acc

    def normed_chunks(cur, slot, gain, use):
        piece[slot] = cur
        part = jnp.sum(cur * cur, axis=-1, keepdims=True)
        stat[slot] = jnp.broadcast_to(part, (rows, LANES))
        sent = []
        for k in range(1, n_tp):
            cp = remote(stat.at[slot], stats.at[k - 1], st_ssem.at[k - 1], st_rsem.at[k - 1], tp=tp_at(k))
            cp.start()
            sent.append(cp)
        for k in range(1, n_tp):
            cp = remote(piece.at[slot], full.at[k - 1], ag_ssem.at[k - 1], ag_rsem.at[k - 1], tp=tp_at(k))
            cp.start()
            sent.append(cp)
        tot = stat[slot]
        for k in range(1, n_tp):
            sent[k - 1].wait_recv()
            tot = tot + stats[k - 1]
        inv = lax.rsqrt(tot * (1.0 / (n_tp * wide)) + NORM_EPS)
        for k in range(n_tp):
            if k == 0:
                v = cur
            else:
                j = FROM[k] - 1
                remote(piece.at[slot], full.at[j], ag_ssem.at[j], ag_rsem.at[j], tp=tp_at(k)).wait_recv()
                v = full[j]
            g = gain_f[gain, tp_at(k)]
            x = [v[:, i * LANES:(i + 1) * LANES] * inv * g[i:i + 1, :] for i in range(per)]
            use(k, jnp.concatenate(x, axis=1).astype(BF))
        for cp in sent:
            cp.wait_send()

    def gate_up(layer, cur, slot, gain):
        def use(k, x):
            n = layer * n_tp + k
            for cp in chunk_copies(n):
                cp.wait()
            out = jnp.dot(x, chunk_b[n % CHUNK_SLOTS], preferred_element_type=F32)
            if k == 0:
                acc_s[...] = out
            else:
                acc_s[...] += out
            if k + CHUNK_SLOTS < n_tp:
                start_chunks(n + CHUNK_SLOTS, n + CHUNK_SLOTS + 1)

        normed_chunks(cur, slot, gain, use)
        gate = acc_s[:, :mlp].astype(BF).astype(F32)
        up = acc_s[:, mlp:].astype(BF).astype(F32)
        act[...] = (gate * jax.nn.sigmoid(gate) * up).astype(BF)

    def load_down(layer):
        for i in range(n_x):
            down_copy(layer, i).start()

    def load_cross_mlp():
        start_chunks(n_tp, n_tp + CHUNK_SLOTS)
        load_down(1)

    def down(layer):
        def product(i):
            down_copy(layer, i).wait()
            return jnp.dot(act[...], down_b[i], preferred_element_type=F32)

        return reduce_scatter(product, load_cross_mlp if layer == 0 else None)

    def wo_product(i):
        return jnp.dot(ob[...], wo_b[:, pl.ds(pl.multiple_of(chip_at(i) * 2 * wide, LANES), 2 * wide)],
                       preferred_element_type=F32)

    def rounded(v):
        return v.astype(BF).astype(F32)

    def row_scale(i):
        sub = lax.broadcasted_iota(jnp.int32, (rows, LANES), 0)
        out = jnp.zeros((rows, LANES), jnp.int32)
        for r in range(rows):
            out = jnp.where(sub == r, mask_sm[r0 + r], out)
        return (jnp.tanh(jnp.full((rows, LANES), gate_sm[i], F32)) * out.astype(F32))[:, 0:1]

    wo_copy.wait()
    acc = reduce_scatter(wo_product, lambda: load_down(0))
    hid_copy.wait()
    gate_up(0, rounded(hid_b[...].astype(F32) + acc), 0, 0)
    woc_copy.start()
    qc_copy.start()
    kc_copy.start()
    vc_copy.start()
    acc = down(0)

    qc_copy.wait()
    q_parts = []

    def use_q(k, x):
        w = qc_b[pl.ds(pl.multiple_of(tp_at(k) * wide, wide), wide), :]
        out = jnp.dot(x, w, preferred_element_type=F32)
        q_parts[:] = [out if k == 0 else q_parts[0] + out]

    normed_chunks(rounded(piece[0] + acc), 1, 1, use_q)
    for h in range(heads):
        v = rounded(q_parts[0][:, h * hd:(h + 1) * hd])
        inv = lax.rsqrt(jnp.mean(v * v, axis=-1, keepdims=True) + NORM_EPS)
        of[h] = rounded(v * inv * qn_ref[...].astype(F32))
    kc_copy.wait()
    vc_copy.wait()
    n_vis = kc_b.shape[1]
    rmod = lax.broadcasted_iota(jnp.int32, (heads * gr, n_vis), 0) % gr
    for g in range(rows // gr):
        qg = jnp.concatenate([of[h, g * gr:(g + 1) * gr] for h in range(heads)], axis=0).astype(BF)
        s = jnp.zeros((heads * gr, n_vis), F32)
        for i in range(gr):
            s_i = lax.dot_general(qg, kc_b[g * gr + i], NT_DIMS, preferred_element_type=F32)
            s = jnp.where(rmod == i, s_i, s)
        valid = xv_ref[g * gr:(g + 1) * gr, :]
        ok = jnp.concatenate([valid] * heads, axis=0) > 0
        s = jnp.where(ok, s * scale, NEG_BIG)
        m = jnp.max(s, axis=-1, keepdims=True)
        pr = jnp.where(ok, jnp.exp(s - m), 0.0)
        l = jnp.sum(pr, axis=-1, keepdims=True)
        o = jnp.zeros((heads * gr, hd), F32)
        for i in range(gr):
            o = o + jnp.dot(jnp.where(rmod == i, pr, 0.0).astype(BF), vc_b[g * gr + i], preferred_element_type=F32)
        o = o / l
        for h in range(heads):
            of[h, g * gr:(g + 1) * gr] = o[h * gr:(h + 1) * gr]
    for h in range(heads):
        ob[:, h * hd:(h + 1) * hd] = of[h].astype(BF)
    woc_copy.wait()
    acc = reduce_scatter(wo_product)

    gate_up(1, rounded(piece[1] + row_scale(0) * acc), 0, 2)
    acc = down(1)
    fin[cc, sp, xx] = rounded(piece[0] + row_scale(1) * acc)

    half = rows // 2
    top = pl.ds(0, half)
    bot = pl.ds(half, half)

    def hop_x(src_sp, src_x, part, dx, ssem, rsem):
        blk = fin.at[cc, src_sp, src_x, part]
        return remote(blk, blk, ssem, rsem, tp=((xx + dx) % n_x) * 2 + cc)

    def hop_y(src_sp, src_x, part, dy, ssem, rsem):
        blk = fin.at[cc, src_sp, src_x, part]
        return remote(blk, blk, ssem, rsem, sp=(sp + dy) % n_sp)

    across = []

    def hop_core(src_sp, src_x, *part):
        blk = fin.at[(cc, src_sp, src_x) + part]
        i = len(across)
        cp = remote(blk, blk, fc_ssem.at[i], fc_rsem.at[i], tp=xx * 2 + (1 - cc))
        cp.start()
        across.append(cp)

    steps = (2, 1, 3)
    first = []
    for i, d in enumerate(steps):
        cx = hop_x(sp, xx, top, d, fd_ssem.at[0, i], fd_rsem.at[0, i])
        cy = hop_y(sp, xx, bot, d, fd_ssem.at[1, i], fd_rsem.at[1, i])
        cx.start()
        cy.start()
        first.append((cx, cy))
    second = []

    def forward(a, from_x, from_y):
        for i, d in enumerate(steps):
            cy = hop_y(sp, from_x, top, d, ff_ssem.at[0, a, i], ff_rsem.at[0, a, i])
            cx = hop_x(from_y, xx, bot, d, ff_ssem.at[1, a, i], ff_rsem.at[1, a, i])
            cy.start()
            cx.start()
            second.append((cx, from_y, (xx + n_x - d) % n_x, cy, (sp + n_sp - d) % n_sp, from_x))

    forward(0, xx, sp)
    hop_core(sp, xx)
    for a, i in ((1, 1), (2, 2), (3, 0)):
        cx, cy = first[i]
        from_x = (xx + n_x - steps[i]) % n_x
        from_y = (sp + n_sp - steps[i]) % n_sp
        cx.wait_recv()
        cy.wait_recv()
        forward(a, from_x, from_y)
        hop_core(sp, from_x, top)
        hop_core(from_y, xx, bot)
    for cx, b_sp, b_x, cy, t_sp, t_x in second:
        cx.wait_recv()
        hop_core(b_sp, b_x, bot)
        cy.wait_recv()
        hop_core(t_sp, t_x, top)
    for cx, cy in first:
        cx.wait_send()
        cy.wait_send()
    for cx, _, _, cy, _, _ in second:
        cx.wait_send()
        cy.wait_send()
    for cp in across:
        cp.wait()
    for c in range(2):
        for s in range(n_sp):
            for x in range(n_x):
                j = x * 2 + c
                out_ref[s * rows:(s + 1) * rows, j * wide:(j + 1) * wide] = fin[c, s, x].astype(BF)


def step_phase(mask, gates, part, gains, qnorm, xvalid, hid, weights, kc, vc, *, n_sp, n_tp, heads, scale):
    all_rows, hidden = hid.shape
    rows = all_rows // n_sp
    wide = hidden // n_tp
    mlp = weights[1].shape[1]
    n_vis, hd = kc.shape[1], kc.shape[2]
    vm = pl.BlockSpec(memory_space=pltpu.VMEM)
    anys = pl.BlockSpec(memory_space=pl.ANY)
    dma = pltpu.SemaphoreType.DMA
    n_x = n_tp // 2
    peers = n_tp - 1
    return pl.pallas_call(
        functools.partial(step_kernel, n_sp=n_sp, n_tp=n_tp, heads=heads, scale=scale),
        out_shape=jax.ShapeDtypeStruct((all_rows, hidden), BF),
        in_specs=[pl.BlockSpec(memory_space=pltpu.SMEM)] * 2 + [anys] * 18,
        out_specs=vm,
        scratch_shapes=[
            pltpu.VMEM(weights[0].shape, BF),
            pltpu.VMEM((CHUNK_SLOTS, wide, 2 * mlp), BF),
            pltpu.VMEM(weights[4].shape, BF),
            pltpu.VMEM((n_x, mlp, 2 * wide), BF),
            pltpu.VMEM((rows, n_vis, hd), BF), pltpu.VMEM((rows, n_vis, hd), BF),
            pltpu.VMEM((rows, wide), BF),
            pltpu.VMEM((n_sp - 1, rows, part.shape[1]), F32),
            pltpu.VMEM((n_tp, rows, wide), F32), pltpu.VMEM((peers, rows, wide), F32),
            pltpu.VMEM((2, rows, wide), F32),
            pltpu.VMEM((peers, rows, wide), F32),
            pltpu.VMEM((2, rows, LANES), F32), pltpu.VMEM((peers, rows, LANES), F32),
            pltpu.VMEM((rows, 2 * mlp), F32),
            pltpu.VMEM((rows, mlp), BF),
            pltpu.VMEM((rows, heads * hd), BF),
            pltpu.VMEM((heads, rows, hd), F32),
            pltpu.VMEM((2, n_sp, n_x, rows, wide), F32),
            pltpu.VMEM(part.shape, F32), pltpu.VMEM((3,) + gains[0].shape, BF),
            pltpu.VMEM((3, n_tp, wide // LANES, LANES), F32), pltpu.VMEM(qnorm.shape, BF),
            pltpu.VMEM((rows, n_vis), jnp.int32), dma((6,)),
            dma, dma((CHUNK_SLOTS, 2)), dma, dma((n_x,)), dma((2,)), dma,
            dma((n_sp - 1,)), dma((n_sp - 1,)), dma((peers + 1,)), dma((peers,)), dma((peers,)), dma((peers,)),
            dma((peers,)), dma((peers,)),
            dma((2, 3)), dma((2, 3)), dma((2, 4, 3)), dma((2, 4, 3)), dma((31,)), dma((31,)),
        ],
        compiler_params=pltpu.CompilerParams(collective_id=1, has_side_effects=True, vmem_limit_bytes=67043328),
        name="decode_step",
    )(mask, gates, part, *gains, qnorm, xvalid, hid, *weights, kc, vc)


def solution(mesh):
    cache_spec = P('dp', 'sp', 'tp', None)
    cross_spec = P('dp', None, 'tp', None)
    row_spec = P('dp', None)
    vec_spec = P('dp')
    full_spec = P(None)
    col_spec = P(None, 'tp')
    split_rows = P('tp', None)
    in_specs = (row_spec, vec_spec, cache_spec, cache_spec, cross_spec, cross_spec, row_spec, vec_spec,
                full_spec, col_spec, col_spec, col_spec, split_rows, full_spec, col_spec, col_spec, split_rows,
                full_spec, col_spec, full_spec, split_rows, full_spec, full_spec, col_spec, col_spec, split_rows)
    out_specs = (row_spec, cache_spec, cache_spec)
    n_sp = mesh.shape['sp']
    n_tp = mesh.shape['tp']

    def local_step(hidden, new_pos, k_self, v_self, k_cross, v_cross, xvalid, rowmask,
                   self_attn_norm, self_wq, self_wk, self_wv, self_wo, self_mlp_norm,
                   self_wgate, self_wup, self_wdown, cross_attn_norm, cross_wq, cross_qnorm,
                   cross_wo, cross_gates, cross_mlp_norm, cross_wgate, cross_wup, cross_wdown):
        batch_rows = hidden.shape[0]
        len_local = k_self.shape[1]
        head_dim = k_self.shape[3]
        heads = self_wq.shape[1] // head_dim
        scale = head_dim ** -0.5
        flat = (batch_rows, len_local, head_dim)
        lanes = (-1, LANES)
        part, ko, vo = self_phase(new_pos, hidden, self_attn_norm.reshape(lanes), self_wq, self_wk, self_wv,
                                  k_self.reshape(flat), v_self.reshape(flat), scale=scale)
        gains = tuple(g.reshape(lanes) for g in (self_mlp_norm, cross_attn_norm, cross_mlp_norm))
        weights = (self_wo, self_wgate, self_wup, self_wdown, cross_wq, cross_wo, cross_wgate, cross_wup, cross_wdown)
        cflat = (batch_rows, k_cross.shape[1], head_dim)
        h4 = step_phase(rowmask, cross_gates, part, gains, cross_qnorm.reshape(lanes), xvalid,
                        hidden, weights, k_cross.reshape(cflat), v_cross.reshape(cflat),
                        n_sp=n_sp, n_tp=n_tp, heads=heads, scale=scale)
        return h4, ko.reshape(k_self.shape), vo.reshape(v_self.shape)

    return jax.shard_map(local_step, mesh=mesh, in_specs=in_specs, out_specs=out_specs, check_vma=False)
```

time: 122 us -> 90.6 us (0.74)
  local copies, waits for them, and re-layouts: 18.6 us -> 1.97 us
  Pallas kernels: 98.6 us -> 87.8 us
  other arithmetic: 2.98 us -> 0 us
    pallas_call x1, Pallas kernels: 90.1 us -> 79.7 us  [step_phase(): pl.pallas_call(functools.partial(step_kernel, n_sp=n_sp, n_tp=n_tp, heads...]
    unnamed x15 -> x1, local copies, waits for them, and re-layouts: 11.3 us -> 1.97 us
    broadcast_in_dim x7 -> x0, local copies, waits for them, and re-layouts: 6.13 us -> none  [the longest x2 1.37 us: local_step(): jnp.broadcast_to(rowmask.astype(F32)[:, None], (batch_rows, LANES))]
    mul x1 -> x0, other arithmetic: 1.95 us -> none  [local_step(): gate_vals[1] * row_scale]
where the time goes in v2:
time: 90.6 us; the launch traced here: 90.4 us
  Pallas kernels  87.8 us (97%)
  local copies, waits for them, and re-layouts  1.97 us (2%)
    pallas_call x1, Pallas kernels, step_phase(): pl.pallas_call(functools.partial(step_kernel, n_sp=n_sp, n_tp=n_tp, heads...  79.7 us
    pallas_call x1, Pallas kernels, self_phase(): pl.pallas_call(functools.partial(self_kernel, chunks=chunks, heads=heads,...  8.13 us
    unnamed x1, local copies, waits for them, and re-layouts  1.97 us

profile of v2, /device:TPU:97, one launch (start us, length us, event | category | flops | bytes accessed | tf_op | source)
XLA Modules:
  0.0 90.4 jit_solution(6434196129692213611)
XLA Ops:
  0.6 8.1 %self_attention.1 = (f32[64,640]{1,0:T(8,128)}, bf16[4096,128]{1,0:T(8,128)(2,1)}, bf16[4096,128]{1,0:T(8,128)(2,1)}) custom-call(s32[64]{0:T(128)} %pos_sm.1, f32[8,128]{1,0:T(8,128)} %constant.2.clone.freq_hbm, bf16[64,5120]{1,0:T(8,128)(2,1)} %hid_hbm.3, bf16[40,128]{1,0:T(8,128)(2,1)} %bitcast.19, bf16[5120,512]{1,0:T(8,128)(2,1)} %wq_hbm.1, ...), custom_call_target="tpu_custom_call" | custom-call | tf_op jit(solution)/shard_map/self_attention/pallas_call | solution.py:172
  8.8 79.7 %decode_step.1 = bf16[64,5120]{1,0:T(8,128)(2,1)} custom-call(s32[64]{0:T(128)} %mask_sm.1, f32[2]{0:T(128)} %gate_sm.1, f32[64,640]{1,0:T(8,128)} %get-tuple-element.6.part_hbm, bf16[40,128]{1,0:T(8,128)(2,1)} %bitcast.20, bf16[40,128]{1,0:T(8,128)(2,1)} %bitcast.21, bf16[40,128]{1,0:T(8,128)(2,1)} %bitcast.22, bf16[1,128]{1,0:T(2,128)(2,1)} %bitcast.23, ...), custom_call_target="tpu_custom_call" | custom-call | tf_op jit(solution)/shard_map/decode_step/pallas_call | solution.py:534
  88.4 2.0 %copy.33 = bf16[64,5120]{1,0:T(8,128)(2,1)} copy(bf16[64,5120]{1,0:T(8,128)(2,1)} %decode_step.1) | data formatting | bytes 1310720

commit v3 on v2

--- a/solution.py
+++ b/solution.py
@@ -20,7 +20,7 @@
 F32 = jnp.float32
 LANES = 128
 GROUP_ROWS = 8
-CHUNK_SLOTS = 5
+CHUNK_SLOTS = 6
 NT_DIMS = (((1,), (1,)), ((), ()))
 ORDER = ((0, 0), (0, 1), (1, 0), (3, 0), (1, 1), (3, 1), (2, 0), (2, 1))
 FROM = (0, 1, 3, 2, 5, 4, 6, 7)
@@ -41,8 +41,8 @@
 
 
 def self_kernel(pos_sm, freq_hbm, hid_hbm, g_hbm, wq_hbm, wk_hbm, wv_hbm, ks_hbm, vs_hbm,
-                part_hbm, ko_hbm, vo_hbm,
-                freq_b, hid_b, g_b, xb, w_b, wk_b, wv_b, kb, vb, q_s, kn_s, vn_s, lp_s, s_s, part_b,
+                part_b, ko_hbm, vo_hbm,
+                freq_b, hid_b, g_b, xb, w_b, wk_b, wv_b, kb, vb, q_s, kn_s, vn_s, lp_s, s_s,
                 i_sem, w_sem, c_sem, o_sem, *, chunks, heads, scale):
     rows, hidden = hid_b.shape
     hd = LANES
@@ -150,9 +150,6 @@
             stat = jnp.where(lane == h, m[hs], stat)
             stat = jnp.where(lane == heads + h, l[hs], stat)
         part_b[rs, qw:] = stat
-    p_out = pltpu.make_async_copy(part_b, part_hbm, o_sem.at[2])
-    p_out.start()
-    p_out.wait()
     k_out.wait()
     v_out.wait()
 
@@ -173,7 +170,7 @@
         functools.partial(self_kernel, chunks=chunks, heads=heads, scale=scale),
         out_shape=(jax.ShapeDtypeStruct(pshape, F32), cache, cache),
         in_specs=[pl.BlockSpec(memory_space=pltpu.SMEM)] + [anys] * 8,
-        out_specs=(anys, anys, anys),
+        out_specs=(pl.BlockSpec(memory_space=pltpu.VMEM), anys, anys),
         scratch_shapes=[
             pltpu.VMEM(freq.shape, F32), pltpu.VMEM((rows, hidden), BF), pltpu.VMEM(gain.shape, BF),
             pltpu.VMEM((rows, hidden), BF), pltpu.VMEM(wq.shape, BF),
@@ -181,20 +178,20 @@
             pltpu.VMEM(ks.shape, BF), pltpu.VMEM(vs.shape, BF),
             pltpu.VMEM((heads, rows, hd), F32), pltpu.VMEM((rows, hd), F32), pltpu.VMEM((rows, hd), F32),
             pltpu.VMEM((rows, LANES), jnp.int32),
-            pltpu.VMEM((rows // GROUP_ROWS, heads * GROUP_ROWS, GROUP_ROWS * tlen), F32), pltpu.VMEM(pshape, F32),
+            pltpu.VMEM((rows // GROUP_ROWS, heads * GROUP_ROWS, GROUP_ROWS * tlen), F32),
             pltpu.SemaphoreType.DMA((5,)), pltpu.SemaphoreType.DMA((chunks,)), pltpu.SemaphoreType.DMA((2,)),
-            pltpu.SemaphoreType.DMA((3,)),
+            pltpu.SemaphoreType.DMA((2,)),
         ],
         compiler_params=pltpu.CompilerParams(vmem_limit_bytes=60 << 20),
         name="self_attention",
     )(pos, freq, hid, gain, wq, wk, wv, ks, vs)
 
 
-def step_kernel(mask_sm, gate_sm, part_hbm, g2_hbm, g3_hbm, g4_hbm, qn_hbm, xv_hbm,
+def step_kernel(mask_sm, gate_sm, part_b, g2_hbm, g3_hbm, g4_hbm, qn_hbm, xv_hbm,
                 hid_hbm, wo_hbm, wg_hbm, wu_hbm, wd_hbm, wqc_hbm, woc_hbm, wgc_hbm, wuc_hbm, wdc_hbm, kc_hbm, vc_hbm,
                 out_ref,
-                wo_b, chunk_b, qc_b, down_b, kc_b, vc_b, hid_b, comb, sbuf, rbuf, piece, full, stat, stats, acc_s, act, ob, of,
-                fin, part_ref, gain_b, gain_f, qn_ref, xv_ref, small_sem,
+                wo_b, chunk_b, qc_b, down_b, kc_b, vc_b, hid_b, comb, sbuf, rbuf, piece, full, stat, stats, acc_s, act, ob,
+                fin, gain_b, gain_f, qn_ref, xv_ref, small_sem,
                 wo_sem, chunk_sem, qc_sem, down_sem, kv_sem, hid_sem, cs_sem, cr_sem, rs_ssem, rs_rsem, ag_ssem, ag_rsem,
                 st_ssem, st_rsem, fd_ssem, fd_rsem, ff_ssem, ff_rsem, fc_ssem, fc_rsem, *, n_sp, n_tp, heads, scale):
     sp = lax.axis_index("sp")
@@ -218,6 +215,12 @@
         return pltpu.make_async_remote_copy(src_ref=src, dst_ref=dst, send_sem=ssem, recv_sem=rsem,
                                             device_id=dev, device_id_type=MESH)
 
+    bar = pltpu.get_barrier_semaphore()
+    for j in range(1, n_sp):
+        pl.semaphore_signal(bar, inc=1, device_id={"sp": (sp + j) % n_sp}, device_id_type=MESH)
+    for k in range(1, n_tp):
+        pl.semaphore_signal(bar, inc=1, device_id={"tp": tp_at(k)}, device_id_type=MESH)
+
     def chunk_copies(n):
         slot = n % CHUNK_SLOTS
         a, b = ((wg_hbm, wu_hbm), (wgc_hbm, wuc_hbm))[n // n_tp]
@@ -245,45 +248,37 @@
         hid_hbm.at[pl.ds(r0, rows), pl.ds(pl.multiple_of(tp * wide, LANES), wide)], hid_b, hid_sem)
     kc_copy = pltpu.make_async_copy(kc_hbm.at[pl.ds(r0, rows)], kc_b, kv_sem.at[0])
     vc_copy = pltpu.make_async_copy(vc_hbm.at[pl.ds(r0, rows)], vc_b, kv_sem.at[1])
-    small = [pltpu.make_async_copy(part_hbm, part_ref, small_sem.at[0]),
-             pltpu.make_async_copy(g2_hbm, gain_b.at[0], small_sem.at[1]),
+    small = [pltpu.make_async_copy(g2_hbm, gain_b.at[0], small_sem.at[1]),
              pltpu.make_async_copy(g3_hbm, gain_b.at[1], small_sem.at[2]),
              pltpu.make_async_copy(g4_hbm, gain_b.at[2], small_sem.at[3]),
              pltpu.make_async_copy(qn_hbm, qn_ref, small_sem.at[4]),
              pltpu.make_async_copy(xv_hbm.at[pl.ds(r0, rows)], xv_ref, small_sem.at[5])]
     for cp in small:
         cp.start()
-
-    bar = pltpu.get_barrier_semaphore()
-    for j in range(1, n_sp):
-        pl.semaphore_signal(bar, inc=1, device_id={"sp": (sp + j) % n_sp}, device_id_type=MESH)
-    for k in range(1, n_tp):
-        pl.semaphore_signal(bar, inc=1, device_id={"tp": tp_at(k)}, device_id_type=MESH)
-
     wo_copy.start()
     hid_copy.start()
     start_chunks(0, 3)
+    pl.semaphore_wait(bar, n_sp - 1 + n_tp - 1)
+
+    sends = []
+    for i, j in enumerate((2, 1, 3)):
+        peer = (sp + j) % n_sp
+        cp = remote(part_b.at[pl.ds(pl.multiple_of(peer * rows, rows), rows)], comb.at[i],
+                    cs_sem.at[i], cr_sem.at[i], sp=peer)
+        cp.start()
+        sends.append(cp)
+    start_chunks(3, CHUNK_SLOTS)
     for cp in small:
         cp.wait()
     for i in range(3):
         g_all = gain_b[i].astype(F32)
         for j in range(n_tp):
             gain_f[i, j] = g_all[j * per:(j + 1) * per, :]
-    pl.semaphore_wait(bar, n_sp - 1 + n_tp - 1)
-
-    sends = []
-    for i, j in enumerate((2, 1, 3)):
-        peer = (sp + j) % n_sp
-        cp = remote(part_ref.at[pl.ds(pl.multiple_of(peer * rows, rows), rows)], comb.at[i],
-                    cs_sem.at[i], cr_sem.at[i], sp=peer)
-        cp.start()
-        sends.append(cp)
-    start_chunks(3, CHUNK_SLOTS)
     for cp in sends:
         cp.wait()
-    own = part_ref[pl.ds(r0, rows), :]
+    qw = heads * hd
+    own = part_b[pl.ds(r0, rows), :]
     blocks = [own] + [comb[j] for j in range(n_sp - 1)]
-    qw = heads * hd
     for h in range(heads):
         ms = [b[:, qw + h:qw + h + 1] for b in blocks]
         top = functools.reduce(jnp.maximum, ms)
@@ -292,62 +287,88 @@
         num = sum(b[:, h * hd:(h + 1) * hd] * f for b, f in zip(blocks, fs))
         ob[:, h * hd:(h + 1) * hd] = (num / den).astype(BF)
 
-    def reduce_scatter(product, then=None):
+    whole = ((0, 0, rows),)
+    halves = ((0, 0, rows // 2), (1, rows // 2, rows // 2))
+    last = 2 * (n_x - 1)
+
+    def reduce_send(product, parts):
         sent = []
         for i in range(n_x):
             out = product(i)
-            sbuf[2 * i] = out[:, :wide]
-            sbuf[2 * i + 1] = out[:, wide:]
+            lo = parts[0][1]
+            n = out.shape[0]
+            sbuf[2 * i, lo:lo + n] = out[:, :wide]
+            sbuf[2 * i + 1, lo:lo + n] = out[:, wide:]
             if i < n_x - 1:
-                for c in range(2):
-                    cp = remote(sbuf.at[2 * i + c], rbuf.at[2 * i + cc], rs_ssem.at[2 * i + c], rs_rsem.at[2 * i + cc],
-                                tp=chip_at(i) * 2 + c)
-                    cp.start()
-                    sent.append(cp)
-        last = 2 * (n_x - 1)
-        cp = remote(sbuf.at[last + 1 - cc], rbuf.at[last], rs_ssem.at[last], rs_rsem.at[last], tp=xx * 2 + 1 - cc)
-        cp.start()
-        sent.append(cp)
+                for h, r, n in parts:
+                    for c in range(2):
+                        cp = remote(sbuf.at[2 * i + c, pl.ds(r, n)], rbuf.at[2 * i + cc, pl.ds(r, n)],
+                                    rs_ssem.at[h, 2 * i + c], rs_rsem.at[h, 2 * i + cc], tp=chip_at(i) * 2 + c)
+                        cp.start()
+                        sent.append(cp)
+        for h, r, n in parts:
+            cp = remote(sbuf.at[last + 1 - cc, pl.ds(r, n)], rbuf.at[last, pl.ds(r, n)], rs_ssem.at[h, last],
+                        rs_rsem.at[h, last], tp=xx * 2 + 1 - cc)
+            cp.start()
+            sent.append(cp)
+        return sent
+
+    def reduce_wait(part):
+        h, r, n = part
+        acc = sbuf[last + cc, r:r + n]
+        for j in (6, 2, 3, 4, 5, 0, 1):
+            remote(sbuf.at[j, pl.ds(r, n)], rbuf.at[j, pl.ds(r, n)], rs_ssem.at[h, j], rs_rsem.at[h, j],
+                   tp=xx * 2 + 1 - cc).wait_recv()
+            acc = acc + rbuf[j, r:r + n]
+        return acc
+
+    def done(sent):
+        for cp in sent:
+            cp.wait_send()
+
+    def reduce_scatter(product, then=None):
+        sent = reduce_send(product, whole)
         if then is not None:
             then()
-        acc = sbuf[last + cc]
-        for j in (6, 2, 3, 4, 5, 0, 1):
-            remote(sbuf.at[j], rbuf.at[j], rs_ssem.at[j], rs_rsem.at[j], tp=xx * 2 + 1 - cc).wait_recv()
-            acc = acc + rbuf[j]
-        for cp in sent:
-            cp.wait_send()
+        acc = reduce_wait(whole[0])
+        done(sent)
         return acc
 
-    def normed_chunks(cur, slot, gain, use):
-        piece[slot] = cur
-        part = jnp.sum(cur * cur, axis=-1, keepdims=True)
-        stat[slot] = jnp.broadcast_to(part, (rows, LANES))
+    def share_send(cur, slot, part):
+        h, r, n = part
+        rs = pl.ds(r, n)
+        piece[slot, r:r + n] = cur
+        stat[slot, r:r + n] = jnp.broadcast_to(jnp.sum(cur * cur, axis=-1, keepdims=True), (n, LANES))
         sent = []
         for k in range(1, n_tp):
-            cp = remote(stat.at[slot], stats.at[k - 1], st_ssem.at[k - 1], st_rsem.at[k - 1], tp=tp_at(k))
+            cp = remote(stat.at[slot, rs], stats.at[k - 1, rs], st_ssem.at[h, k - 1], st_rsem.at[h, k - 1], tp=tp_at(k))
             cp.start()
             sent.append(cp)
         for k in range(1, n_tp):
-            cp = remote(piece.at[slot], full.at[k - 1], ag_ssem.at[k - 1], ag_rsem.at[k - 1], tp=tp_at(k))
+            cp = remote(piece.at[slot, rs], full.at[k - 1, rs], ag_ssem.at[h, k - 1], ag_rsem.at[h, k - 1], tp=tp_at(k))
             cp.start()
             sent.append(cp)
-        tot = stat[slot]
+        return sent
+
+    def share_use(cur, slot, part, gain, use):
+        h, r, n = part
+        rs = pl.ds(r, n)
+        tot = stat[slot, r:r + n]
         for k in range(1, n_tp):
-            sent[k - 1].wait_recv()
-            tot = tot + stats[k - 1]
+            remote(stat.at[slot, rs], stats.at[k - 1, rs], st_ssem.at[h, k - 1], st_rsem.at[h, k - 1],
+                   tp=tp_at(k)).wait_recv()
+            tot = tot + stats[k - 1, r:r + n]
         inv = lax.rsqrt(tot * (1.0 / (n_tp * wide)) + NORM_EPS)
         for k in range(n_tp):
             if k == 0:
                 v = cur
             else:
                 j = FROM[k] - 1
-                remote(piece.at[slot], full.at[j], ag_ssem.at[j], ag_rsem.at[j], tp=tp_at(k)).wait_recv()
-                v = full[j]
+                remote(piece.at[slot, rs], full.at[j, rs], ag_ssem.at[h, j], ag_rsem.at[h, j], tp=tp_at(k)).wait_recv()
+                v = full[j, r:r + n]
             g = gain_f[gain, tp_at(k)]
             x = [v[:, i * LANES:(i + 1) * LANES] * inv * g[i:i + 1, :] for i in range(per)]
             use(k, jnp.concatenate(x, axis=1).astype(BF))
-        for cp in sent:
-            cp.wait_send()
 
     def gate_up(layer, cur, slot, gain):
         def use(k, x):
@@ -362,7 +383,9 @@
             if k + CHUNK_SLOTS < n_tp:
                 start_chunks(n + CHUNK_SLOTS, n + CHUNK_SLOTS + 1)
 
-        normed_chunks(cur, slot, gain, use)
+        sent = share_send(cur, slot, whole[0])
+        share_use(cur, slot, whole[0], gain, use)
+        done(sent)
         gate = acc_s[:, :mlp].astype(BF).astype(F32)
         up = acc_s[:, mlp:].astype(BF).astype(F32)
         act[...] = (gate * jax.nn.sigmoid(gate) * up).astype(BF)
@@ -380,10 +403,10 @@
             down_copy(layer, i).wait()
             return jnp.dot(act[...], down_b[i], preferred_element_type=F32)
 
-        return reduce_scatter(product, load_cross_mlp if layer == 0 else None)
-
-    def wo_product(i):
-        return jnp.dot(ob[...], wo_b[:, pl.ds(pl.multiple_of(chip_at(i) * 2 * wide, LANES), 2 * wide)],
+        return product
+
+    def wo_product(i, r=0, n=rows):
+        return jnp.dot(ob[r:r + n, :], wo_b[:, pl.ds(pl.multiple_of(chip_at(i) * 2 * wide, LANES), 2 * wide)],
                        preferred_element_type=F32)
 
     def rounded(v):
@@ -404,32 +427,43 @@
     qc_copy.start()
     kc_copy.start()
     vc_copy.start()
-    acc = down(0)
-
+    sent_d = reduce_send(down(0), halves)
+    load_cross_mlp()
+
+    cur, sent_g = [], []
+    for part in halves:
+        h, r, n = part
+        cur.append(rounded(piece[0, r:r + n] + reduce_wait(part)))
+        sent_g += share_send(cur[h], 1, part)
+    done(sent_d)
     qc_copy.wait()
-    q_parts = []
-
-    def use_q(k, x):
-        w = qc_b[pl.ds(pl.multiple_of(tp_at(k) * wide, wide), wide), :]
-        out = jnp.dot(x, w, preferred_element_type=F32)
-        q_parts[:] = [out if k == 0 else q_parts[0] + out]
-
-    normed_chunks(rounded(piece[0] + acc), 1, 1, use_q)
-    for h in range(heads):
-        v = rounded(q_parts[0][:, h * hd:(h + 1) * hd])
-        inv = lax.rsqrt(jnp.mean(v * v, axis=-1, keepdims=True) + NORM_EPS)
-        of[h] = rounded(v * inv * qn_ref[...].astype(F32))
     kc_copy.wait()
     vc_copy.wait()
+    woc_copy.wait()
     n_vis = kc_b.shape[1]
     rmod = lax.broadcasted_iota(jnp.int32, (heads * gr, n_vis), 0) % gr
-    for g in range(rows // gr):
-        qg = jnp.concatenate([of[h, g * gr:(g + 1) * gr] for h in range(heads)], axis=0).astype(BF)
+    sent_o = []
+    for part in halves:
+        g, r, _ = part
+        q_parts = []
+
+        def use_q(k, x):
+            w = qc_b[pl.ds(pl.multiple_of(tp_at(k) * wide, wide), wide), :]
+            out = jnp.dot(x, w, preferred_element_type=F32)
+            q_parts[:] = [out if k == 0 else q_parts[0] + out]
+
+        share_use(cur[g], 1, part, 1, use_q)
+        qs = []
+        for h in range(heads):
+            v = rounded(q_parts[0][:, h * hd:(h + 1) * hd])
+            inv = lax.rsqrt(jnp.mean(v * v, axis=-1, keepdims=True) + NORM_EPS)
+            qs.append(rounded(v * inv * qn_ref[...].astype(F32)))
+        qg = jnp.concatenate(qs, axis=0).astype(BF)
         s = jnp.zeros((heads * gr, n_vis), F32)
         for i in range(gr):
-            s_i = lax.dot_general(qg, kc_b[g * gr + i], NT_DIMS, preferred_element_type=F32)
+            s_i = lax.dot_general(qg, kc_b[r + i], NT_DIMS, preferred_element_type=F32)
             s = jnp.where(rmod == i, s_i, s)
-        valid = xv_ref[g * gr:(g + 1) * gr, :]
+        valid = xv_ref[r:r + gr, :]
         ok = jnp.concatenate([valid] * heads, axis=0) > 0
         s = jnp.where(ok, s * scale, NEG_BIG)
         m = jnp.max(s, axis=-1, keepdims=True)
@@ -437,17 +471,17 @@
         l = jnp.sum(pr, axis=-1, keepdims=True)
         o = jnp.zeros((heads * gr, hd), F32)
         for i in range(gr):
-            o = o + jnp.dot(jnp.where(rmod == i, pr, 0.0).astype(BF), vc_b[g * gr + i], preferred_element_type=F32)
+            o = o + jnp.dot(jnp.where(rmod == i, pr, 0.0).astype(BF), vc_b[r + i], preferred_element_type=F32)
         o = o / l
         for h in range(heads):
-            of[h, g * gr:(g + 1) * gr] = o[h * gr:(h + 1) * gr]
-    for h in range(heads):
-        ob[:, h * hd:(h + 1) * hd] = of[h].astype(BF)
-    woc_copy.wait()
-    acc = reduce_scatter(wo_product)
+            ob[r:r + gr, h * hd:(h + 1) * hd] = o[h * gr:(h + 1) * gr].astype(BF)
+        sent_o += reduce_send(functools.partial(wo_product, r=r, n=gr), (part,))
+    done(sent_g)
+    acc = jnp.concatenate([reduce_wait(part) for part in halves], axis=0)
+    done(sent_o)
 
     gate_up(1, rounded(piece[1] + row_scale(0) * acc), 0, 2)
-    acc = down(1)
+    acc = reduce_scatter(down(1))
     fin[cc, sp, xx] = rounded(piece[0] + row_scale(1) * acc)
 
     half = rows // 2
@@ -531,10 +565,11 @@
     dma = pltpu.SemaphoreType.DMA
     n_x = n_tp // 2
     peers = n_tp - 1
+    pwide = part.shape[1]
     return pl.pallas_call(
         functools.partial(step_kernel, n_sp=n_sp, n_tp=n_tp, heads=heads, scale=scale),
         out_shape=jax.ShapeDtypeStruct((all_rows, hidden), BF),
-        in_specs=[pl.BlockSpec(memory_space=pltpu.SMEM)] * 2 + [anys] * 18,
+        in_specs=[pl.BlockSpec(memory_space=pltpu.SMEM)] * 2 + [vm] + [anys] * 17,
         out_specs=vm,
         scratch_shapes=[
             pltpu.VMEM(weights[0].shape, BF),
@@ -543,7 +578,7 @@
             pltpu.VMEM((n_x, mlp, 2 * wide), BF),
             pltpu.VMEM((rows, n_vis, hd), BF), pltpu.VMEM((rows, n_vis, hd), BF),
             pltpu.VMEM((rows, wide), BF),
-            pltpu.VMEM((n_sp - 1, rows, part.shape[1]), F32),
+            pltpu.VMEM((n_sp - 1, rows, pwide), F32),
             pltpu.VMEM((n_tp, rows, wide), F32), pltpu.VMEM((peers, rows, wide), F32),
             pltpu.VMEM((2, rows, wide), F32),
             pltpu.VMEM((peers, rows, wide), F32),
@@ -551,14 +586,13 @@
             pltpu.VMEM((rows, 2 * mlp), F32),
             pltpu.VMEM((rows, mlp), BF),
             pltpu.VMEM((rows, heads * hd), BF),
-            pltpu.VMEM((heads, rows, hd), F32),
             pltpu.VMEM((2, n_sp, n_x, rows, wide), F32),
-            pltpu.VMEM(part.shape, F32), pltpu.VMEM((3,) + gains[0].shape, BF),
+            pltpu.VMEM((3,) + gains[0].shape, BF),
             pltpu.VMEM((3, n_tp, wide // LANES, LANES), F32), pltpu.VMEM(qnorm.shape, BF),
             pltpu.VMEM((rows, n_vis), jnp.int32), dma((6,)),
             dma, dma((CHUNK_SLOTS, 2)), dma, dma((n_x,)), dma((2,)), dma,
-            dma((n_sp - 1,)), dma((n_sp - 1,)), dma((peers + 1,)), dma((peers,)), dma((peers,)), dma((peers,)),
-            dma((peers,)), dma((peers,)),
+            dma((n_sp - 1,)), dma((n_sp - 1,)), dma((2, peers)), dma((2, peers)), dma((2, peers)), dma((2, peers)),
+            dma((2, peers)), dma((2, peers)),
             dma((2, 3)), dma((2, 3)), dma((2, 4, 3)), dma((2, 4, 3)), dma((31,)), dma((31,)),
         ],
         compiler_params=pltpu.CompilerParams(collective_id=1, has_side_effects=True, vmem_limit_bytes=67043328),

time: 90.6 us -> 87 us (0.960)
  Pallas kernels: 87.8 us -> 84.2 us
    pallas_call x1, Pallas kernels: 79.7 us -> 76.1 us  [step_phase(): pl.pallas_call(functools.partial(step_kernel, n_sp=n_sp, n_tp=n_tp, heads...]
where the time goes in v3:
time: 87 us; the launch traced here: 86.8 us
  Pallas kernels  84.2 us (97%)
  local copies, waits for them, and re-layouts  1.97 us (2%)
    pallas_call x1, Pallas kernels, step_phase(): pl.pallas_call(functools.partial(step_kernel, n_sp=n_sp, n_tp=n_tp, heads...  76.1 us
    pallas_call x1, Pallas kernels, self_phase(): pl.pallas_call(functools.partial(self_kernel, chunks=chunks, heads=heads,...  8.12 us
    unnamed x1, local copies, waits for them, and re-layouts  1.97 us

profile of v3, /device:TPU:97, one launch (start us, length us, event | category | flops | bytes accessed | tf_op | source)
XLA Modules:
  0.0 86.8 jit_solution(1821004882931111687)
XLA Ops:
  0.6 8.1 %self_attention.1 = (f32[64,640]{1,0:T(8,128)}, bf16[4096,128]{1,0:T(8,128)(2,1)}, bf16[4096,128]{1,0:T(8,128)(2,1)}) custom-call(s32[64]{0:T(128)} %pos_sm.1, f32[8,128]{1,0:T(8,128)} %constant.2.clone.freq_hbm, bf16[64,5120]{1,0:T(8,128)(2,1)} %hid_hbm.3, bf16[40,128]{1,0:T(8,128)(2,1)} %bitcast.19, bf16[5120,512]{1,0:T(8,128)(2,1)} %wq_hbm.1, ...), custom_call_target="tpu_custom_call" | custom-call | tf_op jit(solution)/shard_map/self_attention/pallas_call | solution.py:169
  8.8 76.1 %decode_step.1 = bf16[64,5120]{1,0:T(8,128)(2,1)} custom-call(s32[64]{0:T(128)} %mask_sm.1, f32[2]{0:T(128)} %gate_sm.1, f32[64,640]{1,0:T(8,128)} %get-tuple-element.6.part_b, bf16[40,128]{1,0:T(8,128)(2,1)} %bitcast.20, bf16[40,128]{1,0:T(8,128)(2,1)} %bitcast.21, bf16[40,128]{1,0:T(8,128)(2,1)} %bitcast.22, bf16[1,128]{1,0:T(2,128)(2,1)} %bitcast.23, ...), custom_call_target="tpu_custom_call" | custom-call | tf_op jit(solution)/shard_map/decode_step/pallas_call | solution.py:569
  84.9 2.0 %copy.33 = bf16[64,5120]{1,0:T(8,128)(2,1)} copy(bf16[64,5120]{1,0:T(8,128)(2,1)} %decode_step.1) | data formatting | bytes 1310720

commit v4 on v3

--- a/solution.py
+++ b/solution.py
@@ -57,11 +57,6 @@
              pltpu.make_async_copy(ks_hbm, kb, c_sem.at[0]), pltpu.make_async_copy(vs_hbm, vb, c_sem.at[1])]
     for cp in kv_in:
         cp.start()
-    loads = []
-    for i in range(chunks):
-        sl = pl.ds(i * kc, kc)
-        loads.append(pltpu.make_async_copy(wq_hbm.at[sl], w_b.at[sl], w_sem.at[i]))
-        loads[-1].start()
     for cp in small:
         cp.wait()
     acc = jnp.zeros((rows, LANES), F32)
@@ -73,6 +68,11 @@
     for c in range(hidden // LANES):
         sl = slice(c * LANES, (c + 1) * LANES)
         xb[:, sl] = (hid_b[:, sl].astype(F32) * inv * g_all[c:c + 1, :]).astype(BF)
+    loads = []
+    for i in range(chunks):
+        sl = pl.ds(i * kc, kc)
+        loads.append(pltpu.make_async_copy(wq_hbm.at[sl], w_b.at[sl], w_sem.at[i]))
+        loads[-1].start()
     gr = GROUP_ROWS
     sub = lax.broadcasted_iota(jnp.int32, (gr, LANES), 0)
     pos_rows = []
@@ -241,6 +241,10 @@
         return pltpu.make_async_copy(src.at[:, pl.ds(pl.multiple_of(chip_at(i) * 2 * wide, LANES), 2 * wide)],
                                      down_b.at[i], down_sem.at[i])
 
+    def load_down(layer):
+        for i in range(n_x):
+            down_copy(layer, i).start()
+
     wo_copy = pltpu.make_async_copy(wo_hbm, wo_b, wo_sem)
     woc_copy = pltpu.make_async_copy(woc_hbm, wo_b, wo_sem)
     qc_copy = pltpu.make_async_copy(wqc_hbm, qc_b, qc_sem)
@@ -276,6 +280,7 @@
             gain_f[i, j] = g_all[j * per:(j + 1) * per, :]
     for cp in sends:
         cp.wait()
+    load_down(0)
     qw = heads * hd
     own = part_b[pl.ds(r0, rows), :]
     blocks = [own] + [comb[j] for j in range(n_sp - 1)]
@@ -390,10 +395,6 @@
         up = acc_s[:, mlp:].astype(BF).astype(F32)
         act[...] = (gate * jax.nn.sigmoid(gate) * up).astype(BF)
 
-    def load_down(layer):
-        for i in range(n_x):
-            down_copy(layer, i).start()
-
     def load_cross_mlp():
         start_chunks(n_tp, n_tp + CHUNK_SLOTS)
         load_down(1)
@@ -420,7 +421,7 @@
         return (jnp.tanh(jnp.full((rows, LANES), gate_sm[i], F32)) * out.astype(F32))[:, 0:1]
 
     wo_copy.wait()
-    acc = reduce_scatter(wo_product, lambda: load_down(0))
+    acc = reduce_scatter(wo_product)
     hid_copy.wait()
     gate_up(0, rounded(hid_b[...].astype(F32) + acc), 0, 0)
     woc_copy.start()
@@ -505,7 +506,7 @@
         cp.start()
         across.append(cp)
 
-    steps = (2, 1, 3)
+    steps = (1, 3, 2)
     first = []
     for i, d in enumerate(steps):
         cx = hop_x(sp, xx, top, d, fd_ssem.at[0, i], fd_rsem.at[0, i])
@@ -525,7 +526,7 @@
 
     forward(0, xx, sp)
     hop_core(sp, xx)
-    for a, i in ((1, 1), (2, 2), (3, 0)):
+    for a, i in ((1, 0), (2, 1), (3, 2)):
         cx, cy = first[i]
         from_x = (xx + n_x - steps[i]) % n_x
         from_y = (sp + n_sp - steps[i]) % n_sp

time: 87 us -> 85.6 us (0.984)
  Pallas kernels: 84.2 us -> 82.9 us
    pallas_call x1, Pallas kernels: 8.12 us -> 6.98 us  [self_phase(): pl.pallas_call(functools.partial(self_kernel, chunks=chunks, heads=heads,...]
where the time goes in v4:
time: 85.6 us; the launch traced here: 85.5 us
  Pallas kernels  82.9 us (97%)
  local copies, waits for them, and re-layouts  1.97 us (2%)
    pallas_call x1, Pallas kernels, step_phase(): pl.pallas_call(functools.partial(step_kernel, n_sp=n_sp, n_tp=n_tp, heads...  75.9 us
    pallas_call x1, Pallas kernels, self_phase(): pl.pallas_call(functools.partial(self_kernel, chunks=chunks, heads=heads,...  6.98 us
    unnamed x1, local copies, waits for them, and re-layouts  1.97 us

profile of v4, /device:TPU:97, one launch (start us, length us, event | category | flops | bytes accessed | tf_op | source)
XLA Modules:
  0.0 85.5 jit_solution(16272913482202955388)
XLA Ops:
  0.6 7.0 %self_attention.1 = (f32[64,640]{1,0:T(8,128)}, bf16[4096,128]{1,0:T(8,128)(2,1)}, bf16[4096,128]{1,0:T(8,128)(2,1)}) custom-call(s32[64]{0:T(128)} %pos_sm.1, f32[8,128]{1,0:T(8,128)} %constant.2.clone.freq_hbm, bf16[64,5120]{1,0:T(8,128)(2,1)} %hid_hbm.3, bf16[40,128]{1,0:T(8,128)(2,1)} %bitcast.19, bf16[5120,512]{1,0:T(8,128)(2,1)} %wq_hbm.1, ...), custom_call_target="tpu_custom_call" | custom-call | tf_op jit(solution)/shard_map/self_attention/pallas_call | solution.py:169
  7.6 75.9 %decode_step.1 = bf16[64,5120]{1,0:T(8,128)(2,1)} custom-call(s32[64]{0:T(128)} %mask_sm.1, f32[2]{0:T(128)} %gate_sm.1, f32[64,640]{1,0:T(8,128)} %get-tuple-element.6.part_b, bf16[40,128]{1,0:T(8,128)(2,1)} %bitcast.20, bf16[40,128]{1,0:T(8,128)(2,1)} %bitcast.21, bf16[40,128]{1,0:T(8,128)(2,1)} %bitcast.22, bf16[1,128]{1,0:T(2,128)(2,1)} %bitcast.23, ...), custom_call_target="tpu_custom_call" | custom-call | tf_op jit(solution)/shard_map/decode_step/pallas_call | solution.py:570
  83.5 2.0 %copy.33 = bf16[64,5120]{1,0:T(8,128)(2,1)} copy(bf16[64,5120]{1,0:T(8,128)(2,1)} %decode_step.1) | data formatting | bytes 1310720
